TPU v7x, 32 devices: a whole 2x2x4 slice. The times are simulated.
32 devices in a mesh: expert: 8 (over z, core), row: 4 (over y, x).
Axes of the slice: x: 2, y: 2, z: 4, core: 2. Of those that a mesh axis runs over, the one named last changes fastest.
Arguments:
- grads: bfloat16 [8, 7168, 2048], P('expert', 'row')
- basis: bfloat16 [8, 7168, 256], P('expert', 'row'), may hold values from -0.0625 to 0.0625
- loads: int32 [8], P('expert'), may hold values from 1 to 1, as said below
- flags: int32 [8], P('expert'), may hold values 0 or 1
Outputs:
- new_basis: float32 [8, 7168, 256], P('expert', 'row')
- rotated: float32 [8, 256, 2048], P('expert', None, 'row')
Inputs may be any that keep to these rules, and one draw needn't show every extreme that they name: Slots 0 to loads[d] - 1 of expert-axis index d are live and hold experts; the others are empty. Some index has all 1 slots live.
All inputs are finite; a program needn't handle non-finite values. No bound on the sum of `flags` on one device may be relied on, other than what follows from the above.
Results may differ from a plain program's by a relative error of at most 0.006.
Values sent between devices are 32-bit elements; how exact they have to be, the bound alone decides.
A program may use at most 64 MiB of HBM per device.

v0:
```python
import functools

import jax
import jax.numpy as jnp
from jax import lax
from jax.experimental import pallas as pl
from jax.experimental.pallas import tpu as pltpu
from jax.sharding import PartitionSpec as P

PANEL = 16
HIGHEST = lax.Precision.HIGHEST
F32 = jnp.float32
BF16 = jnp.bfloat16


def dot(a, b, precision=None):
    return lax.dot_general(a, b, (((1,), (0,)), ((), ())), precision=precision, preferred_element_type=F32)


def dot_t(a, b, precision=None):
    return lax.dot_general(a, b, (((1,), (1,)), ((), ())), precision=precision, preferred_element_type=F32)


def pieces_of(x, count):
    pieces = []
    for _ in range(count):
        pieces.append(x.astype(BF16))
        x = x - pieces[-1].astype(F32)
    return pieces


def first_bit(mask, order):
    for phase, bit in enumerate(order):
        if mask >> bit & 1:
            return phase
    return len(order)


def panel_step(work, step):
    size = work.shape[0]
    panel = work[0:PANEL, :]
    rows = lax.broadcasted_iota(jnp.int32, (PANEL, 128), 0)
    lanes = lax.broadcasted_iota(jnp.int32, (PANEL, 128), 1)
    columns = [jnp.broadcast_to(panel[:, j : j + 1], (PANEL, 128)) for j in range(PANEL)]
    pieces = [panel[:, at : at + 128] for at in range(0, size, 128)]
    unit = (rows == lanes).astype(F32)
    root = jnp.zeros((PANEL, 128), F32)
    for j in range(PANEL):
        inverse_root = lax.rsqrt(columns[j][j : j + 1, :])
        root = jnp.where(rows == j, inverse_root, root)
        factor = jnp.where(rows > j, columns[j] * (inverse_root * inverse_root), 0.0)
        for k in range(j + 1, PANEL):
            columns[k] = columns[k] - factor * columns[k][j : j + 1, :]
        pieces = [piece - factor * piece[j : j + 1, :] for piece in pieces]
        unit = unit - factor * unit[j : j + 1, :]
    scaled = [root * piece for piece in pieces]
    full = jnp.concatenate([jnp.where(lanes < PANEL, root * unit, scaled[0])] + scaled[1:], axis=1)
    where = lax.broadcasted_iota(jnp.int32, (PANEL, size), 1)
    open_columns = jnp.logical_and(where >= PANEL, where < size - PANEL * step)
    left = jnp.where(open_columns, jnp.concatenate(scaled, axis=1), 0.0)
    update = dot(left.T, full, HIGHEST)
    body = work[PANEL:, :]
    ahead = lax.broadcasted_iota(jnp.int32, body.shape, 1) < PANEL
    rest = jnp.where(ahead, 0.0, body) - update[PANEL:, :]
    work[0 : size - PANEL, :] = pltpu.roll(rest, size - PANEL, 1)
    work[size - PANEL :, :] = pltpu.roll(full, size - PANEL, 1)


def panel_steps(work, begin, end):
    def body(step, carry):
        panel_step(work, step)
        return carry

    lax.fori_loop(begin, end, body, 0)


def lower_of(work):
    shape = work.shape
    below = lax.broadcasted_iota(jnp.int32, shape, 1) <= lax.broadcasted_iota(jnp.int32, shape, 0)
    return jnp.where(below, work[...], 0.0)


def kernel(
    n, experts, entries, g_hbm, b_ref, live_ref, refresh_ref, fresh_ref, rot_ref,
    g_ref, g_sem, bt, part, land, part2, land2, full, inner, power_t, rough, tops, lows, top_rows, low_rows, work, inv1,
    gram, gram_land, total, total_land,
    s_rs, r_rs, s_ag, r_ag, s_rs2, r_rs2, s_gr, r_gr, s_tot, r_tot,
):
    depth, wide = g_ref.shape
    bits = n.bit_length() - 1
    expert_bits = experts.bit_length() - 1
    size = b_ref.shape[1]
    half = size // 2
    block = wide // n
    me = lax.axis_index("row")
    my_expert = lax.axis_index("expert")
    orders = [tuple(range(bits)), tuple(reversed(range(bits)))]

    def other(index, mask):
        at = index
        for bit in range(max(bits, expert_bits)):
            if mask >> bit & 1:
                at = at + (1 - 2 * (lax.rem(index // (1 << bit), 2))) * (1 << bit)
        return at

    def partner(bit):
        return {"row": other(me, 1 << bit), "expert": my_expert}

    def expert_partner(bit):
        return {"row": me, "expert": other(my_expert, 1 << bit)}

    everyone = [partner(b) for b in range(bits)] + [expert_partner(b) for b in range(expert_bits)]
    barrier = pltpu.get_barrier_semaphore()
    for peer in everyone:
        pl.semaphore_signal(barrier, inc=1, device_id=peer, device_id_type=pl.DeviceIdType.MESH)

    def columns(mask):
        return pl.ds(pl.multiple_of(other(me, mask) * block, block), block)

    def load(mask):
        return pltpu.make_async_copy(g_hbm.at[:, columns(mask)], g_ref.at[:, columns(mask)], g_sem.at[mask])

    def copy(src, dst, send, recv, to):
        return pltpu.make_async_remote_copy(
            src_ref=src, dst_ref=dst, send_sem=send, recv_sem=recv,
            device_id=to, device_id_type=pl.DeviceIdType.MESH,
        )

    moves = []
    for phase in range(bits):
        for h in range(2):
            order = orders[h]
            masks = [m for m in range(n) if first_bit(m, order) == phase]
            masks.sort(key=lambda m: first_bit(m & ~(1 << order[phase]), order))
            moves.append([(h, phase, m, m & ~(1 << order[phase])) for m in masks])
    schedule = []
    for phase in range(bits):
        a, b = moves[2 * phase], moves[2 * phase + 1]
        schedule.append([move for pair in zip(a, b) for move in pair])
    slot = {}
    for phase_moves in schedule:
        for h, phase, m, there in phase_moves:
            slot[h, phase, there] = len(slot)

    def halving(part_ref, land_ref, sends, recvs):
        def make(h, phase, m, there):
            at = slot[h, phase, there]
            return copy(part_ref.at[h, m], land_ref.at[at], sends.at[at], recvs.at[at], partner(orders[h][phase]))

        def absorb(h, phase, m):
            at = slot[h, phase, m]
            back = m | 1 << orders[h][phase]
            make(h, phase, back, m).wait_recv()
            part_ref[h, m] = part_ref[h, m] + land_ref[at]

        return make, absorb

    def begin(left_ref, part_ref, make, ensure=lambda m: None):
        started = set()
        for move in schedule[0]:
            h, _, m, _ = move
            ensure(m)
            part_ref[h, m] = dot(left_ref[h * half : (h + 1) * half, :], g_ref[:, columns(m)])
            make(*move).start()
            started.add((h, m))
        for m in range(n):
            ensure(m)
            for h in range(2):
                if (h, m) not in started:
                    part_ref[h, m] = dot(left_ref[h * half : (h + 1) * half, :], g_ref[:, columns(m)])

    def forward(make, absorb):
        for phase in range(1, bits):
            for move in schedule[phase]:
                h, _, m, _ = move
                for earlier in range(phase):
                    absorb(h, earlier, m)
                make(*move).start()

    def finish(make, absorb):
        for phase in range(bits):
            for h in range(2):
                absorb(h, phase, 0)
        for phase_moves in schedule:
            for move in phase_moves:
                make(*move).wait_send()

    def gram_exchange(use, between=None):
        for phase in range(bits):
            made = []
            for h in range(2):
                rows = slice(h * half, (h + 1) * half)
                made.append(copy(
                    gram.at[use, phase, rows], gram_land.at[use, phase, rows],
                    s_gr.at[use, phase, h], r_gr.at[use, phase, h], partner(orders[h][phase]),
                ))
            for item in made:
                item.start()
            if between is not None:
                between(phase)
            for h, item in enumerate(made):
                rows = slice(h * half, (h + 1) * half)
                item.wait_recv()
                gram[use, phase + 1, rows] = gram[use, phase, rows] + gram_land[use, phase, rows]
            for item in made:
                item.wait_send()

    peers = everyone

    def total_copy(at):
        return copy(total.at[at], total_land.at[at], s_tot.at[at], r_tot.at[at], peers[at])

    def total_next(at):
        total_copy(at).wait()
        total[at + 1] = total[at] + total_land[at]
        if at + 1 < len(peers):
            total_copy(at + 1).start()

    make, absorb = halving(part, land, s_rs, r_rs)
    wanted = [move[2] for move in schedule[0]] + list(range(n))
    wanted = sorted(range(n), key=wanted.index)
    for m in wanted:
        load(m).start()

    live = live_ref[0] >= 1
    refresh = refresh_ref[0] == 1

    strip = 128 if depth % 128 == 0 else depth
    for at in range(0, depth, strip):
        bt[:, at : at + strip] = b_ref[at : at + strip, :].T

    pl.semaphore_wait(barrier, len(everyone))

    loaded = []

    def ensure(m):
        if m not in loaded:
            load(m).wait()
            loaded.append(m)

    begin(bt, part, make, ensure)

    def squares_of(step, sums):
        rows = g_ref[pl.ds(pl.multiple_of(step * 16, 16), 16), :].astype(F32)
        square = rows * rows
        for at in range(0, wide, 128):
            sums = sums + square[0:8, at : at + 128] + square[8:16, at : at + 128]
        return sums

    sums = lax.fori_loop(0, depth // 16, squares_of, jnp.zeros((8, 128), F32))
    total_sq = jnp.where(live, jnp.sum(sums), 0.0)
    count = jnp.where(jnp.logical_and(live, me == 0), 1.0, 0.0)
    tile_row = lax.broadcasted_iota(jnp.int32, (8, 128), 0)
    total[0] = jnp.where(tile_row == 0, total_sq, jnp.where(tile_row == 1, count, 0.0))
    total_copy(0).start()

    forward(make, absorb)
    finish(make, absorb)

    mine = jnp.concatenate([part[0, 0], part[1, 0]], axis=0).astype(BF16)
    gram[0, 0] = dot_t(mine, mine)
    gram_exchange(0)

    spread = []
    for h in range(2):
        order = tuple(reversed(orders[h]))
        held = [0]
        for bit in order:
            for m in list(held):
                spread.append((h, bit, m))
                held.append(m | 1 << bit)
    number = {(h, m | 1 << bit): at for at, (h, bit, m) in enumerate(spread)}

    def spread_copy(h, bit, m):
        at = number[h, m | 1 << bit]
        src = part.at[h, 0] if m == 0 else full.at[h, m]
        return copy(src, full.at[h, m | 1 << bit], s_ag.at[at], r_ag.at[at], partner(bit))

    arrived = set()

    def take(h, m):
        if m == 0 or (h, m) in arrived:
            return
        arrived.add((h, m))
        bit = next(b for (hh, b, mm) in spread if hh == h and mm | 1 << b == m)
        spread_copy(h, bit, m & ~(1 << bit)).wait_recv()

    def keep(h, m):
        source = part[h, 0] if m == 0 else full[h, m]
        inner[columns(m), h * half : (h + 1) * half] = source.T.astype(BF16)

    rank = {0: [], 1: []}
    for h, bit, m in spread:
        if m == 0:
            rank[h].append((h, bit, m))
    for pair in zip(rank[0], rank[1]):
        for item in pair:
            spread_copy(*item).start()
    work[...] = gram[0, bits]
    panels = size // PANEL
    panel_steps(work, 0, panels // 2)
    total_next(0)
    for h, bit, m in sorted((s for s in spread if s[2]), key=lambda s: bin(s[2]).count("1")):
        take(h, m)
        spread_copy(h, bit, m).start()
    panel_steps(work, panels // 2, panels)
    inv1[...] = lower_of(work)
    tile = 256 if depth % 256 == 0 else 64
    masks = sorted(range(n), key=lambda v: bin(v).count("1"))
    for m in masks:
        for h in range(2):
            take(h, m)
            keep(h, m)
        if m == masks[-1]:
            break
        for at in range(0, depth, tile):
            rows = slice(at, at + tile)
            term = dot(g_ref[rows, columns(m)], inner[columns(m), :])
            rough[rows, :] = term if m == 0 else rough[rows, :] + term
    for at in range(0, depth, tile):
        rows = slice(at, at + tile)
        last = dot(g_ref[rows, columns(masks[-1])], inner[columns(masks[-1]), :])
        power_t[:, rows] = (rough[rows, :] + last).astype(BF16).T
    one, two, three = pieces_of(inv1[...], 3)
    for at in range(0, depth, tile):
        rows = slice(at, at + tile)
        block_t = power_t[:, rows]
        once = dot(three, block_t) + dot(two, block_t) + dot(one, block_t)
        tops[:, rows], lows[:, rows] = pieces_of(once, 2)
    crossed = dot_t(tops[...], lows[...])
    gram[1, 0] = dot_t(tops[...], tops[...]) + (dot_t(lows[...], lows[...]) + (crossed + crossed.T))
    for item in spread:
        spread_copy(*item).wait_send()
    if len(peers) > 1:
        total_next(1)

    make2, absorb2 = halving(part2, land2, s_rs2, r_rs2)

    def cross_part(h, m):
        part2[h, m] = dot(power_t[h * half : (h + 1) * half, :], g_ref[:, columns(m)])

    def beside(phase):
        if phase == 0:
            for h, _, m, _ in schedule[0]:
                cross_part(h, m)
        if phase == bits - 1:
            for move in schedule[0]:
                make2(*move).start()
            started = [(move[0], move[2]) for move in schedule[0]]
            for h, m in [(h, m) for m in range(n) for h in range(2)]:
                if (h, m) not in started:
                    cross_part(h, m)
            for at in range(0, depth, tile):
                rows = slice(at, at + tile)
                top_rows[rows, :] = tops[:, rows].T
                low_rows[rows, :] = lows[:, rows].T

    gram_exchange(1, beside)
    for at in range(2, len(peers) - 1):
        total_next(at)
    work[...] = gram[1, bits]
    panel_steps(work, 0, panels // 2)
    forward(make2, absorb2)
    panel_steps(work, panels // 2, panels)
    inv2 = lower_of(work)
    high, low = pieces_of(inv2.T, 2)
    for at in range(0, depth, tile):
        rows = slice(at, at + tile)
        fresh = dot(low_rows[rows, :], high) + dot(top_rows[rows, :], low) + dot(top_rows[rows, :], high)
        fresh_ref[rows, :] = jnp.where(refresh, fresh, jnp.where(live, b_ref[rows, :].astype(F32), 0.0))
    both = dot(inv2, inv1[...], HIGHEST)
    if len(peers) > 2:
        total_next(len(peers) - 1)
    final = total[len(peers)]
    norm = lax.rsqrt(final[0:1, 0:1] / (final[1:2, 0:1] * entries) + 1e-6)
    finish(make2, absorb2)
    cross = jnp.concatenate([part2[0, 0], part2[1, 0]], axis=0)
    stale = jnp.concatenate([part[0, 0], part[1, 0]], axis=0)
    turned = dot(both, cross, HIGHEST)
    rot_ref[...] = jnp.where(refresh, turned, jnp.where(live, stale, 0.0)) * norm


def on_device(n, experts, grads, basis, loads, flags):
    _, depth, wide = grads.shape
    size = basis.shape[2]
    block = wide // n
    bits = n.bit_length() - 1
    peers = bits + experts.bit_length() - 1
    moves = 2 * (n - 1)
    live = loads
    refresh = jnp.where(loads >= 1, flags, 0)
    vmem = pl.BlockSpec(memory_space=pltpu.VMEM)
    smem = pl.BlockSpec(memory_space=pltpu.SMEM)
    chunk = (size // 2, block)
    dma = pltpu.SemaphoreType.DMA
    new_basis, rotated = pl.pallas_call(
        functools.partial(kernel, n, experts, float(depth * n * wide)),
        out_shape=(
            jax.ShapeDtypeStruct((depth, size), F32),
            jax.ShapeDtypeStruct((size, block), F32),
        ),
        in_specs=[pl.BlockSpec(memory_space=pl.ANY), vmem, smem, smem],
        out_specs=(vmem, vmem),
        scratch_shapes=[
            pltpu.VMEM((depth, wide), BF16),
            pltpu.SemaphoreType.DMA((n,)),
            pltpu.VMEM((size, depth), BF16),
            pltpu.VMEM((2, n, *chunk), F32),
            pltpu.VMEM((moves, *chunk), F32),
            pltpu.VMEM((2, n, *chunk), F32),
            pltpu.VMEM((moves, *chunk), F32),
            pltpu.VMEM((2, n, *chunk), F32),
            pltpu.VMEM((wide, size), BF16),
            pltpu.VMEM((size, depth), BF16),
            pltpu.VMEM((depth, size), F32),
            pltpu.VMEM((size, depth), BF16),
            pltpu.VMEM((size, depth), BF16),
            pltpu.VMEM((depth, size), BF16),
            pltpu.VMEM((depth, size), BF16),
            pltpu.VMEM((size, size), F32),
            pltpu.VMEM((size, size), F32),
            pltpu.VMEM((2, bits + 1, size, size), F32),
            pltpu.VMEM((2, bits, size, size), F32),
            pltpu.VMEM((peers + 1, 8, 128), F32),
            pltpu.VMEM((peers, 8, 128), F32),
            dma((moves,)), dma((moves,)), dma((moves,)), dma((moves,)), dma((moves,)), dma((moves,)),
            dma((2, bits, 2)), dma((2, bits, 2)), dma((peers,)), dma((peers,)),
        ],
        compiler_params=pltpu.CompilerParams(
            collective_id=0, has_side_effects=True, vmem_limit_bytes=58 * 1024 * 1024
        ),
    )(grads[0], basis[0], live, refresh)
    return new_basis[None], rotated[None]


def solution(mesh):
    placed = (P("expert", "row", None), P("expert", "row", None), P("expert"), P("expert"))
    return jax.shard_map(
        functools.partial(on_device, mesh.shape["row"], mesh.shape["expert"]),
        mesh=mesh,
        in_specs=placed,
        out_specs=(P("expert", "row", None), P("expert", None, "row")),
        check_vma=False,
    )
```

profile of v0, /device:TPU:0, one launch (start us, length us, event | category | flops | bytes accessed | tf_op | source)
XLA Modules:
  0.0 89.8 jit_solution(14122672194137465014)
XLA Ops:
  1.9 84.2 %shard_map.59 = (f32[1792,256]{1,0:T(8,128)}, f32[256,512]{1,0:T(8,128)}) custom-call(bf16[1792,2048]{1,0:T(8,128)(2,1)} %bitcast.4, bf16[1792,256]{1,0:T(8,128)(2,1)} %bitcast.6, s32[1]{0:T(128)S(6)} %copy.8.live_ref, s32[1]{0:T(128)S(6)} %select_n.4.refresh_ref), custom_call_target="tpu_custom_call" | custom-call | tf_op jit(solution)/shard_map/pallas_call | solution.py:396
  86.1 0.0 copy-start
  86.1 2.9 %copy.10 = f32[1,1792,256]{2,1,0:T(8,128)} copy(f32[1,1792,256]{2,1,0:T(8,128)} %bitcast.5) | data formatting | bytes 3670016
  89.0 0.0 copy-done
  89.0 0.8 copy.11
Async XLA Ops:
  86.1 2.9 %copy-start = (f32[256,512]{1,0:T(8,128)S(1)}, f32[256,512]{1,0:T(8,128)}, u32[]{:S(2)}) copy-start(f32[256,512]{1,0:T(8,128)} %get-tuple-element.5) | copy-start | bytes 1572868
where the time goes:
time: 90 us; the launch traced here: 89.8 us
  Pallas kernels  84.2 us (94%)
  local copies, waits for them, and re-layouts  3.7 us (4%)
  between operations  1.94 us (2%)
    pallas_call x1, Pallas kernels, on_device(): pl.pallas_call(functools.partial(kernel, n, experts, float(depth * n * wi...  84.2 us
    unnamed x4, local copies, waits for them, and re-layouts  3.7 us

commit v1 on v0

--- a/solution.py
+++ b/solution.py
@@ -82,7 +82,7 @@
 
 def kernel(
     n, experts, entries, g_hbm, b_ref, live_ref, refresh_ref, fresh_ref, rot_ref,
-    g_ref, g_sem, bt, part, land, part2, land2, full, inner, power_t, rough, tops, lows, top_rows, low_rows, work, inv1,
+    g_ref, g_sem, bt, part, land, part2, land2, full, inner, power_t, rough, power, work,
     gram, gram_land, total, total_land,
     s_rs, r_rs, s_ag, r_ag, s_rs2, r_rs2, s_gr, r_gr, s_tot, r_tot,
 ):
@@ -185,23 +185,22 @@
             for move in phase_moves:
                 make(*move).wait_send()
 
-    def gram_exchange(use, between=None):
+    def gram_exchange(between):
         for phase in range(bits):
             made = []
             for h in range(2):
                 rows = slice(h * half, (h + 1) * half)
                 made.append(copy(
-                    gram.at[use, phase, rows], gram_land.at[use, phase, rows],
-                    s_gr.at[use, phase, h], r_gr.at[use, phase, h], partner(orders[h][phase]),
+                    gram.at[phase, rows], gram_land.at[phase, rows],
+                    s_gr.at[phase, h], r_gr.at[phase, h], partner(orders[h][phase]),
                 ))
             for item in made:
                 item.start()
-            if between is not None:
-                between(phase)
+            between(phase)
             for h, item in enumerate(made):
                 rows = slice(h * half, (h + 1) * half)
                 item.wait_recv()
-                gram[use, phase + 1, rows] = gram[use, phase, rows] + gram_land[use, phase, rows]
+                gram[phase + 1, rows] = gram[phase, rows] + gram_land[phase, rows]
             for item in made:
                 item.wait_send()
 
@@ -256,10 +255,6 @@
 
     forward(make, absorb)
     finish(make, absorb)
-
-    mine = jnp.concatenate([part[0, 0], part[1, 0]], axis=0).astype(BF16)
-    gram[0, 0] = dot_t(mine, mine)
-    gram_exchange(0)
 
     spread = []
     for h in range(2):
@@ -296,15 +291,11 @@
     for pair in zip(rank[0], rank[1]):
         for item in pair:
             spread_copy(*item).start()
-    work[...] = gram[0, bits]
     panels = size // PANEL
-    panel_steps(work, 0, panels // 2)
     total_next(0)
     for h, bit, m in sorted((s for s in spread if s[2]), key=lambda s: bin(s[2]).count("1")):
         take(h, m)
         spread_copy(h, bit, m).start()
-    panel_steps(work, panels // 2, panels)
-    inv1[...] = lower_of(work)
     tile = 256 if depth % 256 == 0 else 64
     masks = sorted(range(n), key=lambda v: bin(v).count("1"))
     for m in masks:
@@ -320,15 +311,9 @@
     for at in range(0, depth, tile):
         rows = slice(at, at + tile)
         last = dot(g_ref[rows, columns(masks[-1])], inner[columns(masks[-1]), :])
-        power_t[:, rows] = (rough[rows, :] + last).astype(BF16).T
-    one, two, three = pieces_of(inv1[...], 3)
-    for at in range(0, depth, tile):
-        rows = slice(at, at + tile)
-        block_t = power_t[:, rows]
-        once = dot(three, block_t) + dot(two, block_t) + dot(one, block_t)
-        tops[:, rows], lows[:, rows] = pieces_of(once, 2)
-    crossed = dot_t(tops[...], lows[...])
-    gram[1, 0] = dot_t(tops[...], tops[...]) + (dot_t(lows[...], lows[...]) + (crossed + crossed.T))
+        power[rows, :] = (rough[rows, :] + last).astype(BF16)
+        power_t[:, rows] = power[rows, :].T
+    gram[0] = dot_t(power_t[...], power_t[...])
     for item in spread:
         spread_copy(*item).wait_send()
     if len(peers) > 1:
@@ -350,25 +335,20 @@
             for h, m in [(h, m) for m in range(n) for h in range(2)]:
                 if (h, m) not in started:
                     cross_part(h, m)
-            for at in range(0, depth, tile):
-                rows = slice(at, at + tile)
-                top_rows[rows, :] = tops[:, rows].T
-                low_rows[rows, :] = lows[:, rows].T
-
-    gram_exchange(1, beside)
+
+    gram_exchange(beside)
     for at in range(2, len(peers) - 1):
         total_next(at)
-    work[...] = gram[1, bits]
+    work[...] = gram[bits]
     panel_steps(work, 0, panels // 2)
     forward(make2, absorb2)
     panel_steps(work, panels // 2, panels)
-    inv2 = lower_of(work)
-    high, low = pieces_of(inv2.T, 2)
+    inverse = lower_of(work)
+    turn = pieces_of(inverse.T, 3)
     for at in range(0, depth, tile):
         rows = slice(at, at + tile)
-        fresh = dot(low_rows[rows, :], high) + dot(top_rows[rows, :], low) + dot(top_rows[rows, :], high)
+        fresh = dot(power[rows, :], turn[2]) + dot(power[rows, :], turn[1]) + dot(power[rows, :], turn[0])
         fresh_ref[rows, :] = jnp.where(refresh, fresh, jnp.where(live, b_ref[rows, :].astype(F32), 0.0))
-    both = dot(inv2, inv1[...], HIGHEST)
     if len(peers) > 2:
         total_next(len(peers) - 1)
     final = total[len(peers)]
@@ -376,7 +356,7 @@
     finish(make2, absorb2)
     cross = jnp.concatenate([part2[0, 0], part2[1, 0]], axis=0)
     stale = jnp.concatenate([part[0, 0], part[1, 0]], axis=0)
-    turned = dot(both, cross, HIGHEST)
+    turned = dot(inverse, cross, HIGHEST)
     rot_ref[...] = jnp.where(refresh, turned, jnp.where(live, stale, 0.0)) * norm
 
 
@@ -413,18 +393,14 @@
             pltpu.VMEM((wide, size), BF16),
             pltpu.VMEM((size, depth), BF16),
             pltpu.VMEM((depth, size), F32),
-            pltpu.VMEM((size, depth), BF16),
-            pltpu.VMEM((size, depth), BF16),
-            pltpu.VMEM((depth, size), BF16),
             pltpu.VMEM((depth, size), BF16),
             pltpu.VMEM((size, size), F32),
-            pltpu.VMEM((size, size), F32),
-            pltpu.VMEM((2, bits + 1, size, size), F32),
-            pltpu.VMEM((2, bits, size, size), F32),
+            pltpu.VMEM((bits + 1, size, size), F32),
+            pltpu.VMEM((bits, size, size), F32),
             pltpu.VMEM((peers + 1, 8, 128), F32),
             pltpu.VMEM((peers, 8, 128), F32),
             dma((moves,)), dma((moves,)), dma((moves,)), dma((moves,)), dma((moves,)), dma((moves,)),
-            dma((2, bits, 2)), dma((2, bits, 2)), dma((peers,)), dma((peers,)),
+            dma((bits, 2)), dma((bits, 2)), dma((peers,)), dma((peers,)),
         ],
         compiler_params=pltpu.CompilerParams(
             collective_id=0, has_side_effects=True, vmem_limit_bytes=58 * 1024 * 1024

time: 90 us -> 79.5 us (0.88)
  Pallas kernels: 84.2 us -> 73.6 us
    pallas_call x1, Pallas kernels: 84.2 us -> 73.6 us  [on_device(): pl.pallas_call(functools.partial(kernel, n, experts, float(depth * n * wi...]
where the time goes in v1:
time: 79.5 us; the launch traced here: 79.3 us
  Pallas kernels  73.6 us (93%)
  local copies, waits for them, and re-layouts  3.7 us (5%)
  between operations  1.94 us (2%)
    pallas_call x1, Pallas kernels, on_device(): pl.pallas_call(functools.partial(kernel, n, experts, float(depth * n * wi...  73.6 us
    unnamed x4, local copies, waits for them, and re-layouts  3.7 us

profile of v1, /device:TPU:0, one launch (start us, length us, event | category | flops | bytes accessed | tf_op | source)
XLA Modules:
  0.0 79.3 jit_solution(4820839510935028382)
XLA Ops:
  1.9 73.6 %shard_map.59 = (f32[1792,256]{1,0:T(8,128)}, f32[256,512]{1,0:T(8,128)}) custom-call(bf16[1792,2048]{1,0:T(8,128)(2,1)} %bitcast.4, bf16[1792,256]{1,0:T(8,128)(2,1)} %bitcast.6, s32[1]{0:T(128)S(6)} %copy.8.live_ref, s32[1]{0:T(128)S(6)} %select_n.4.refresh_ref), custom_call_target="tpu_custom_call" | custom-call | tf_op jit(solution)/shard_map/pallas_call | solution.py:376
  75.6 0.0 copy-start
  75.6 2.9 %copy.10 = f32[1,1792,256]{2,1,0:T(8,128)} copy(f32[1,1792,256]{2,1,0:T(8,128)} %bitcast.5) | data formatting | bytes 3670016
  78.5 0.0 copy-done
  78.5 0.8 %copy.11 = f32[1,256,512]{2,1,0:T(8,128)} copy(f32[1,256,512]{2,1,0:T(8,128)S(1)} %bitcast.7) | data formatting | bytes 1048576
Async XLA Ops:
  75.6 2.9 %copy-start = (f32[256,512]{1,0:T(8,128)S(1)}, f32[256,512]{1,0:T(8,128)}, u32[]{:S(2)}) copy-start(f32[256,512]{1,0:T(8,128)} %get-tuple-element.5) | copy-start | bytes 1572868

commit v2 on v1

v2 whole, which is shorter than its diff:
```python
import functools

import jax
import jax.numpy as jnp
from jax import lax
from jax.experimental import pallas as pl
from jax.experimental.pallas import tpu as pltpu
from jax.sharding import PartitionSpec as P

PANEL = 16
HIGHEST = lax.Precision.HIGHEST
F32 = jnp.float32
BF16 = jnp.bfloat16


def dot(a, b, precision=None):
    return lax.dot_general(a, b, (((1,), (0,)), ((), ())), precision=precision, preferred_element_type=F32)


def dot_t(a, b, precision=None):
    return lax.dot_general(a, b, (((1,), (1,)), ((), ())), precision=precision, preferred_element_type=F32)


def pieces_of(x, count):
    pieces = []
    for _ in range(count):
        pieces.append(x.astype(BF16))
        x = x - pieces[-1].astype(F32)
    return pieces


def first_bit(mask, order):
    for phase, bit in enumerate(order):
        if mask >> bit & 1:
            return phase
    return len(order)


def panel_step(work, step):
    size = work.shape[0]
    panel = work[0:PANEL, :]
    rows = lax.broadcasted_iota(jnp.int32, (PANEL, 128), 0)
    lanes = lax.broadcasted_iota(jnp.int32, (PANEL, 128), 1)
    columns = [jnp.broadcast_to(panel[:, j : j + 1], (PANEL, 128)) for j in range(PANEL)]
    pieces = [panel[:, at : at + 128] for at in range(0, size, 128)]
    unit = (rows == lanes).astype(F32)
    root = jnp.zeros((PANEL, 128), F32)
    for j in range(PANEL):
        inverse_root = lax.rsqrt(columns[j][j : j + 1, :])
        root = jnp.where(rows == j, inverse_root, root)
        factor = jnp.where(rows > j, columns[j] * (inverse_root * inverse_root), 0.0)
        for k in range(j + 1, PANEL):
            columns[k] = columns[k] - factor * columns[k][j : j + 1, :]
        pieces = [piece - factor * piece[j : j + 1, :] for piece in pieces]
        unit = unit - factor * unit[j : j + 1, :]
    scaled = [root * piece for piece in pieces]
    full = jnp.concatenate([jnp.where(lanes < PANEL, root * unit, scaled[0])] + scaled[1:], axis=1)
    where = lax.broadcasted_iota(jnp.int32, (PANEL, size), 1)
    open_columns = jnp.logical_and(where >= PANEL, where < size - PANEL * step)
    left = jnp.where(open_columns, jnp.concatenate(scaled, axis=1), 0.0)
    update = dot(left.T, full, HIGHEST)
    body = work[PANEL:, :]
    ahead = lax.broadcasted_iota(jnp.int32, body.shape, 1) < PANEL
    rest = jnp.where(ahead, 0.0, body) - update[PANEL:, :]
    work[0 : size - PANEL, :] = pltpu.roll(rest, size - PANEL, 1)
    work[size - PANEL :, :] = pltpu.roll(full, size - PANEL, 1)


def panel_steps(work, begin, end):
    def body(step, carry):
        panel_step(work, step)
        return carry

    lax.fori_loop(begin, end, body, 0)


def lower_of(work):
    shape = work.shape
    below = lax.broadcasted_iota(jnp.int32, shape, 1) <= lax.broadcasted_iota(jnp.int32, shape, 0)
    return jnp.where(below, work[...], 0.0)


def kernel(
    n, experts, entries, g_hbm, b_hbm, loads_hbm, flags_hbm, fresh_hbm, rot_hbm,
    g_ref, b_ref, bt, part, land, full, inner, rough, power, part2, land2,
    gram_a, gram_a_land, gram_b, gram_b_land, work, fresh, rot, total, total_land, loads, flags,
    g_sem, b_sem, in_sem, out_sem,
    s_rs, r_rs, s_ag, r_ag, s_rs2, r_rs2, s_gr, r_gr, s_tot, r_tot,
):
    _, depth, block = g_ref.shape
    bits = n.bit_length() - 1
    expert_bits = experts.bit_length() - 1
    size = b_ref.shape[1]
    half = size // 2
    sub = half // 2
    me = lax.axis_index("row")
    my_expert = lax.axis_index("expert")
    orders = [tuple(range(bits)), tuple(reversed(range(bits)))]

    def other(index, mask):
        at = index
        for bit in range(max(bits, expert_bits)):
            if mask >> bit & 1:
                at = at + (1 - 2 * (lax.rem(index // (1 << bit), 2))) * (1 << bit)
        return at

    def partner(bit):
        return {"row": other(me, 1 << bit), "expert": my_expert}

    def expert_partner(bit):
        return {"row": me, "expert": other(my_expert, 1 << bit)}

    peers = [partner(b) for b in range(bits)] + [expert_partner(b) for b in range(expert_bits)]
    barrier = pltpu.get_barrier_semaphore()
    for peer in peers:
        pl.semaphore_signal(barrier, inc=1, device_id=peer, device_id_type=pl.DeviceIdType.MESH)

    def load(m):
        columns = pl.ds(pl.multiple_of(other(me, m) * block, block), block)
        return pltpu.make_async_copy(g_hbm.at[:, columns], g_ref.at[m], g_sem.at[m])

    def load_basis(a):
        columns = pl.ds(a * half, half)
        return pltpu.make_async_copy(b_hbm.at[:, columns], b_ref.at[:, columns], b_sem.at[a])

    def copy(src, dst, send, recv, to):
        return pltpu.make_async_remote_copy(
            src_ref=src, dst_ref=dst, send_sem=send, recv_sem=recv,
            device_id=to, device_id_type=pl.DeviceIdType.MESH,
        )

    def strip(h):
        return pl.ds(h * sub, sub)

    schedule = []
    for phase in range(bits):
        lanes = []
        for h in range(2):
            order = orders[h]
            masks = [m for m in range(n) if first_bit(m, order) == phase]
            masks.sort(key=lambda m: first_bit(m & ~(1 << order[phase]), order))
            lanes.append([(h, phase, m, m & ~(1 << order[phase])) for m in masks])
        schedule.append([move for pair in zip(*lanes) for move in pair])
    slot = {}
    for phase_moves in schedule:
        for h, phase, m, there in phase_moves:
            slot[h, phase, there] = len(slot)

    class Halving:
        def __init__(self, a, parts, lands, sends, recvs):
            self.a, self.parts, self.lands, self.sends, self.recvs = a, parts, lands, sends, recvs

        def make(self, h, phase, m, there):
            at = slot[h, phase, there]
            return copy(
                self.parts.at[self.a, m, strip(h)], self.lands.at[self.a, at],
                self.sends.at[self.a, at], self.recvs.at[self.a, at], partner(orders[h][phase]),
            )

        def absorb(self, h, phase, m):
            self.make(h, phase, m | 1 << orders[h][phase], m).wait_recv()
            rows = slice(h * sub, (h + 1) * sub)
            self.parts[self.a, m, rows] = self.parts[self.a, m, rows] + self.lands[self.a, slot[h, phase, m]]

        def send(self, moves):
            for move in moves:
                self.make(*move).start()

        def forward(self):
            for phase in range(1, bits):
                for move in schedule[phase]:
                    for earlier in range(phase):
                        self.absorb(move[0], earlier, move[2])
                    self.make(*move).start()

        def finish(self):
            for phase in range(bits):
                for h in range(2):
                    self.absorb(h, phase, 0)

        def drain(self):
            for phase_moves in schedule:
                for move in phase_moves:
                    self.make(*move).wait_send()

    first = [Halving(a, part, land, s_rs, r_rs) for a in range(2)]
    second = [Halving(a, part2, land2, s_rs2, r_rs2) for a in range(2)]

    spread = []
    for h in range(2):
        held = [0]
        for bit in reversed(orders[h]):
            for m in list(held):
                spread.append((h, bit, m))
                held.append(m | 1 << bit)
    number = {(h, m | 1 << bit): at for at, (h, bit, m) in enumerate(spread)}
    source = {(h, m | 1 << bit): (h, bit, m) for h, bit, m in spread}
    own = [item for pair in zip(*[[s for s in spread if s[0] == h and s[2] == 0] for h in range(2)]) for item in pair]
    relayed = sorted((s for s in spread if s[2]), key=lambda s: bin(s[2]).count("1"))

    def spread_copy(a, h, bit, m):
        at = number[h, m | 1 << bit]
        src = part.at[a, 0, strip(h)] if m == 0 else full.at[a, m, strip(h)]
        return copy(src, full.at[a, m | 1 << bit, strip(h)], s_ag.at[a, at], r_ag.at[a, at], partner(bit))

    arrived = set()

    def take(a, h, m):
        if m and (a, h, m) not in arrived:
            arrived.add((a, h, m))
            spread_copy(a, *source[h, m]).wait_recv()

    def relay(a):
        for h, bit, m in relayed:
            take(a, h, m)
            spread_copy(a, h, bit, m).start()

    tile = 256 if depth % 256 == 0 else 64
    masks = sorted(range(n), key=lambda v: bin(v).count("1"))

    def add_power(a, m):
        for h in range(2):
            take(a, h, m)
        held = part[a, 0] if m == 0 else full[a, m]
        inner[a, m] = held.astype(BF16)
        for at in range(0, depth, tile):
            rows = slice(at, at + tile)
            term = dot_t(inner[a, m], g_ref[m, rows, :])
            if m:
                term = rough[a, :, rows] + term
            if m == masks[-1]:
                power[a * half : (a + 1) * half, rows] = term.astype(BF16)
            else:
                rough[a, :, rows] = term

    grams = [(gram_a, gram_a_land), (gram_b, gram_b_land)]

    def gram_copy(a, phase, h):
        held, landed = grams[a]
        extent = held.shape[1] // 2
        rows = pl.ds(h * extent, extent)
        return copy(
            held.at[phase, rows], landed.at[phase, rows],
            s_gr.at[a, phase, h], r_gr.at[a, phase, h], partner(orders[h][phase]),
        )

    def gram_send(a, phase):
        for h in range(2):
            gram_copy(a, phase, h).start()

    def gram_add(a, phase):
        held, landed = grams[a]
        extent = held.shape[1] // 2
        for h in range(2):
            rows = slice(h * extent, (h + 1) * extent)
            gram_copy(a, phase, h).wait_recv()
            held[phase + 1, rows] = held[phase, rows] + landed[phase, rows]

    def total_copy(at):
        return copy(total.at[at], total_land.at[at], s_tot.at[at], r_tot.at[at], peers[at])

    def total_next(at):
        if at >= len(peers):
            return
        total_copy(at).wait()
        total[at + 1] = total[at] + total_land[at]
        if at + 1 < len(peers):
            total_copy(at + 1).start()

    wanted = [move[2] for move in schedule[0]] + list(range(n))
    wanted = sorted(range(n), key=wanted.index)
    load_basis(0).start()
    load(wanted[0]).start()
    load_basis(1).start()
    for m in wanted[1:]:
        load(m).start()
    small = [
        pltpu.make_async_copy(loads_hbm, loads, in_sem.at[0]),
        pltpu.make_async_copy(flags_hbm, flags, in_sem.at[1]),
    ]
    for item in small:
        item.start()

    span = 128 if depth % 128 == 0 else depth

    def turn_basis(a):
        load_basis(a).wait()
        for at in range(0, depth, span):
            bt[a * half : (a + 1) * half, at : at + span] = b_ref[at : at + span, a * half : (a + 1) * half].T

    turn_basis(0)
    pl.semaphore_wait(barrier, len(peers))
    for m in wanted:
        load(m).wait()
        part[0, m] = dot(bt[0:half, :], g_ref[m])
        first[0].send([move for move in schedule[0] if move[2] == m])
    turn_basis(1)
    for m in wanted:
        part[1, m] = dot(bt[half:size, :], g_ref[m])
    first[0].forward()
    first[1].send(schedule[0])

    for item in small:
        item.wait()
    live = loads[0] >= 1
    refresh = jnp.logical_and(live, flags[0] == 1)

    def squares_of(step, sums):
        rows = pl.ds(pl.multiple_of(step * 16, 16), 16)
        for m in range(n):
            piece = g_ref[m, rows, :].astype(F32)
            sums = sums + piece * piece
        return sums

    sums = lax.fori_loop(0, depth // 16, squares_of, jnp.zeros((16, block), F32))
    total_sq = jnp.where(live, jnp.sum(sums), 0.0)
    count = jnp.where(jnp.logical_and(live, me == 0), 1.0, 0.0)
    tile_row = lax.broadcasted_iota(jnp.int32, (8, 128), 0)
    total[0] = jnp.where(tile_row == 0, total_sq, jnp.where(tile_row == 1, count, 0.0))
    total_copy(0).start()

    first[0].finish()
    for item in own[:2]:
        spread_copy(0, *item).start()
    first[1].forward()
    for item in own[2:]:
        spread_copy(0, *item).start()
    add_power(0, 0)
    relay(0)
    first[1].finish()
    for item in own:
        spread_copy(1, *item).start()
    total_next(0)
    add_power(1, 0)
    for m in masks[1:]:
        add_power(0, m)
    gram_a[0] = dot_t(power[0:half, :], power[0:half, :])
    gram_send(0, 0)

    def cross_part(a):
        for m in wanted:
            part2[a, m] = dot(power[a * half : (a + 1) * half, :], g_ref[m])

    cross_part(0)
    total_next(1)
    relay(1)
    second[0].send(schedule[0][:2])
    for phase in range(bits - 1):
        gram_add(0, phase)
        gram_send(0, phase + 1)
    second[0].send(schedule[0][2:])
    total_next(2)
    for m in masks[1:]:
        add_power(1, m)
    gram_b[0] = dot_t(power[...], power[half:size, :])
    gram_send(1, 0)
    gram_add(0, bits - 1)
    panels = half // PANEL
    work[...] = gram_a[bits]
    panel_steps(work, 0, panels // 2)
    second[0].forward()
    cross_part(1)
    panel_steps(work, panels // 2, panels)
    for phase in range(bits - 1):
        gram_add(1, phase)
        gram_send(1, phase + 1)
    second[1].send(schedule[0])
    total_next(3)

    def write_fresh(a, pieces):
        for at in range(0, depth, tile):
            rows = slice(at, at + tile)
            columns = slice(a * half, (a + 1) * half)
            left = power[0 : (a + 1) * half, rows].T
            value = dot(left, pieces[2]) + dot(left, pieces[1]) + dot(left, pieces[0])
            kept = jnp.where(live, b_ref[rows, columns].astype(F32), 0.0)
            fresh[a, rows, :] = jnp.where(refresh, value, kept)
        fresh_out(a).start()

    def fresh_out(a):
        return pltpu.make_async_copy(fresh.at[a], fresh_hbm.at[:, pl.ds(a * half, half)], out_sem.at[a])

    def rot_out(a):
        rows = pl.ds(a * half, half)
        return pltpu.make_async_copy(rot.at[rows], rot_hbm.at[rows], out_sem.at[2 + a])

    inverse_a = lower_of(work)
    write_fresh(0, pieces_of(inverse_a.T, 3))
    second[0].finish()
    turned_a = dot(inverse_a, part2[0, 0], HIGHEST)
    gram_add(1, bits - 1)
    upper = dot(inverse_a, gram_b[bits, 0:half], HIGHEST)
    work[...] = gram_b[bits, half:size] - dot(upper.T, upper, HIGHEST)
    panel_steps(work, 0, panels // 2)
    second[1].forward()
    panel_steps(work, panels // 2, panels)
    inverse_b = lower_of(work)
    mixed = -dot(inverse_b, dot(upper.T, inverse_a, HIGHEST), HIGHEST)
    write_fresh(1, pieces_of(jnp.concatenate([mixed, inverse_b], axis=1).T, 3))
    partly = dot(mixed, part2[0, 0], HIGHEST)
    for at in range(4, len(peers)):
        total_next(at)
    final = total[len(peers)]
    norm = lax.rsqrt(final[0:1, 0:1] / (final[1:2, 0:1] * entries) + 1e-6)

    def write_rot(a, turned):
        value = jnp.where(refresh, turned, jnp.where(live, part[a, 0], 0.0)) * norm
        rot[a * half : (a + 1) * half, :] = value
        rot_out(a).start()

    write_rot(0, turned_a)
    second[1].finish()
    write_rot(1, partly + dot(inverse_b, part2[1, 0], HIGHEST))
    for a in range(2):
        first[a].drain()
        second[a].drain()
        for item in spread:
            spread_copy(a, *item).wait_send()
        for phase in range(bits):
            for h in range(2):
                gram_copy(a, phase, h).wait_send()
        fresh_out(a).wait()
    for a in range(2):
        rot_out(a).wait()


def on_device(n, experts, grads, basis, loads, flags):
    _, depth, wide = grads.shape
    size = basis.shape[2]
    half = size // 2
    block = wide // n
    bits = n.bit_length() - 1
    peers = bits + experts.bit_length() - 1
    moves = 2 * (n - 1)
    anywhere = pl.BlockSpec(memory_space=pl.ANY)
    chunk = (half // 2, block)
    dma = pltpu.SemaphoreType.DMA
    new_basis, rotated = pl.pallas_call(
        functools.partial(kernel, n, experts, float(depth * n * wide)),
        out_shape=(
            jax.ShapeDtypeStruct((depth, size), F32),
            jax.ShapeDtypeStruct((size, block), F32),
        ),
        in_specs=[anywhere] * 4,
        out_specs=(anywhere, anywhere),
        scratch_shapes=[
            pltpu.VMEM((n, depth, block), BF16),
            pltpu.VMEM((depth, size), BF16),
            pltpu.VMEM((size, depth), BF16),
            pltpu.VMEM((2, n, half, block), F32),
            pltpu.VMEM((2, moves, *chunk), F32),
            pltpu.VMEM((2, n, half, block), F32),
            pltpu.VMEM((2, n, half, block), BF16),
            pltpu.VMEM((2, half, depth), F32),
            pltpu.VMEM((size, depth), BF16),
            pltpu.VMEM((2, n, half, block), F32),
            pltpu.VMEM((2, moves, *chunk), F32),
            pltpu.VMEM((bits + 1, half, half), F32),
            pltpu.VMEM((bits, half, half), F32),
            pltpu.VMEM((bits + 1, size, half), F32),
            pltpu.VMEM((bits, size, half), F32),
            pltpu.VMEM((half, half), F32),
            pltpu.VMEM((2, depth, half), F32),
            pltpu.VMEM((size, block), F32),
            pltpu.VMEM((peers + 1, 8, 128), F32),
            pltpu.VMEM((peers, 8, 128), F32),
            pltpu.SMEM((1,), jnp.int32),
            pltpu.SMEM((1,), jnp.int32),
            dma((n,)), dma((2,)), dma((2,)), dma((4,)),
            dma((2, moves)), dma((2, moves)), dma((2, moves)), dma((2, moves)), dma((2, moves)), dma((2, moves)),
            dma((2, bits, 2)), dma((2, bits, 2)), dma((peers,)), dma((peers,)),
        ],
        compiler_params=pltpu.CompilerParams(
            collective_id=0, has_side_effects=True, vmem_limit_bytes=58 * 1024 * 1024
        ),
    )(grads[0], basis[0], loads, flags)
    return new_basis[None], rotated[None]


def solution(mesh):
    placed = (P("expert", "row", None), P("expert", "row", None), P("expert"), P("expert"))
    return jax.shard_map(
        functools.partial(on_device, mesh.shape["row"], mesh.shape["expert"]),
        mesh=mesh,
        in_specs=placed,
        out_specs=(P("expert", "row", None), P("expert", None, "row")),
        check_vma=False,
    )
```

time: 79.5 us -> 72 us (0.906)
  Pallas kernels: 73.6 us -> 66.2 us
    pallas_call x1, Pallas kernels: 73.6 us -> 66.2 us  [on_device(): pl.pallas_call(functools.partial(kernel, n, experts, float(depth * n * wi...]
where the time goes in v2:
time: 72 us; the launch traced here: 71.8 us
  Pallas kernels  66.2 us (92%)
  local copies, waits for them, and re-layouts  3.7 us (5%)
  between operations  1.94 us (3%)
    pallas_call x1, Pallas kernels, on_device(): pl.pallas_call(functools.partial(kernel, n, experts, float(depth * n * wi...  66.2 us
    unnamed x4, local copies, waits for them, and re-layouts  3.7 us

profile of v2, /device:TPU:0, one launch (start us, length us, event | category | flops | bytes accessed | tf_op | source)
XLA Modules:
  0.0 71.8 jit_solution(16977709023399646217)
XLA Ops:
  1.9 66.2 %shard_map.59 = (f32[1792,256]{1,0:T(8,128)}, f32[256,512]{1,0:T(8,128)}) custom-call(bf16[1792,2048]{1,0:T(8,128)(2,1)} %bitcast.4, bf16[1792,256]{1,0:T(8,128)(2,1)} %bitcast.6, s32[1]{0:T(128)S(6)} %copy.8.loads_hbm, s32[1]{0:T(128)S(6)} %copy.9.flags_hbm), custom_call_target="tpu_custom_call" | custom-call | tf_op jit(solution)/shard_map/pallas_call | solution.py:438
  68.1 0.0 copy-start
  68.1 2.9 %copy.10 = f32[1,1792,256]{2,1,0:T(8,128)} copy(f32[1,1792,256]{2,1,0:T(8,128)} %bitcast.5) | data formatting | bytes 3670016
  71.0 0.0 copy-done
  71.0 0.8 %copy.11 = f32[1,256,512]{2,1,0:T(8,128)} copy(f32[1,256,512]{2,1,0:T(8,128)S(1)} %bitcast.7) | data formatting | bytes 1048576
Async XLA Ops:
  68.1 2.9 %copy-start = (f32[256,512]{1,0:T(8,128)S(1)}, f32[256,512]{1,0:T(8,128)}, u32[]{:S(2)}) copy-start(f32[256,512]{1,0:T(8,128)} %get-tuple-element.5) | copy-start | bytes 1572868

commit v3 on v2

--- a/solution.py
+++ b/solution.py
@@ -8,6 +8,8 @@
 from jax.sharding import PartitionSpec as P
 
 PANEL = 16
+PARTS = 4
+SWAP, ACROSS, OUTWARD = range(3)
 HIGHEST = lax.Precision.HIGHEST
 F32 = jnp.float32
 BF16 = jnp.bfloat16
@@ -81,10 +83,10 @@
 
 
 def kernel(
-    n, experts, entries, g_hbm, b_hbm, loads_hbm, flags_hbm, fresh_hbm, rot_hbm,
+    n, experts, entries, g_hbm, b_hbm, loads, flags, fresh, rot,
     g_ref, b_ref, bt, part, land, full, inner, rough, power, part2, land2,
-    gram_a, gram_a_land, gram_b, gram_b_land, work, fresh, rot, total, total_land, loads, flags,
-    g_sem, b_sem, in_sem, out_sem,
+    gram_a, gram_a_land, gram_b, gram_b_land, work, total, total_land,
+    g_sem, b_sem,
     s_rs, r_rs, s_ag, r_ag, s_rs2, r_rs2, s_gr, r_gr, s_tot, r_tot,
 ):
     _, depth, block = g_ref.shape
@@ -110,10 +112,27 @@
     def expert_partner(bit):
         return {"row": me, "expert": other(my_expert, 1 << bit)}
 
-    peers = [partner(b) for b in range(bits)] + [expert_partner(b) for b in range(expert_bits)]
+    place = my_expert // 2
+    inside = jnp.logical_or(place == 1, place == 2)
+    across = {"row": me, "expert": my_expert + jnp.where(place == 1, 2, -2)}
+    if expert_bits == 3:
+        rounds = [(SWAP, expert_partner(0)), (SWAP, expert_partner(1)), (ACROSS, across), (OUTWARD, expert_partner(1))]
+    else:
+        rounds = [(SWAP, expert_partner(b)) for b in range(expert_bits)]
+    rounds = rounds + [(SWAP, partner(b)) for b in range(bits)]
     barrier = pltpu.get_barrier_semaphore()
-    for peer in peers:
+
+    def greet(peer):
         pl.semaphore_signal(barrier, inc=1, device_id=peer, device_id_type=pl.DeviceIdType.MESH)
+
+    greetings = 0
+    for kind, peer in rounds:
+        if kind == SWAP:
+            greet(peer)
+            greetings += 1
+    if expert_bits == 3:
+        pl.when(inside)(lambda: greet(across))
+        greetings = greetings + inside.astype(jnp.int32)
 
     def load(m):
         columns = pl.ds(pl.multiple_of(other(me, m) * block, block), block)
@@ -257,53 +276,79 @@
             held[phase + 1, rows] = held[phase, rows] + landed[phase, rows]
 
     def total_copy(at):
-        return copy(total.at[at], total_land.at[at], s_tot.at[at], r_tot.at[at], peers[at])
+        return copy(total.at[at], total_land.at[at], s_tot.at[at], r_tot.at[at], rounds[at][1])
+
+    def total_start(at):
+        if at == len(rounds):
+            return
+        if rounds[at][0] == SWAP:
+            total_copy(at).start()
+        else:
+            pl.when(inside)(lambda: total_copy(at).start())
 
     def total_next(at):
-        if at >= len(peers):
+        if at >= len(rounds):
             return
-        total_copy(at).wait()
-        total[at + 1] = total[at] + total_land[at]
-        if at + 1 < len(peers):
-            total_copy(at + 1).start()
+        kind = rounds[at][0]
+
+        def add():
+            total_copy(at).wait()
+            total[at + 1] = total[at] + total_land[at]
+
+        def give():
+            total_copy(at).wait_send()
+            total[at + 1] = total[at]
+
+        def accept():
+            total_copy(at).wait_recv()
+            total[at + 1] = total_land[at]
+
+        if kind == SWAP:
+            add()
+        elif kind == ACROSS:
+            pl.when(inside)(add)
+        else:
+            pl.when(inside)(give)
+            pl.when(jnp.logical_not(inside))(accept)
+        total_start(at + 1)
 
     wanted = [move[2] for move in schedule[0]] + list(range(n))
     wanted = sorted(range(n), key=wanted.index)
     load_basis(0).start()
     load(wanted[0]).start()
+    span = 128 if depth % 128 == 0 else depth
+
+    def turn_basis(a):
+        for at in range(0, depth, span):
+            bt[a * half : (a + 1) * half, at : at + span] = b_ref[at : at + span, a * half : (a + 1) * half].T
+
+    load_basis(0).wait()
     load_basis(1).start()
     for m in wanted[1:]:
         load(m).start()
-    small = [
-        pltpu.make_async_copy(loads_hbm, loads, in_sem.at[0]),
-        pltpu.make_async_copy(flags_hbm, flags, in_sem.at[1]),
-    ]
-    for item in small:
-        item.start()
-
-    span = 128 if depth % 128 == 0 else depth
-
-    def turn_basis(a):
-        load_basis(a).wait()
-        for at in range(0, depth, span):
-            bt[a * half : (a + 1) * half, at : at + span] = b_ref[at : at + span, a * half : (a + 1) * half].T
-
     turn_basis(0)
-    pl.semaphore_wait(barrier, len(peers))
+    pl.semaphore_wait(barrier, greetings)
+
+    def inner_part(a, m):
+        part[a, m] = dot(bt[a * half : (a + 1) * half, :], g_ref[m])
+
+    opening = schedule[0][:2]
+    rest = schedule[0][2:]
     for m in wanted:
         load(m).wait()
-        part[0, m] = dot(bt[0:half, :], g_ref[m])
+        if m == wanted[-1]:
+            load_basis(1).wait()
+            turn_basis(1)
+            inner_part(1, wanted[0])
+            first[1].send(opening)
+        inner_part(0, m)
         first[0].send([move for move in schedule[0] if move[2] == m])
-    turn_basis(1)
-    for m in wanted:
-        part[1, m] = dot(bt[half:size, :], g_ref[m])
-    first[0].forward()
-    first[1].send(schedule[0])
-
-    for item in small:
-        item.wait()
+    for m in wanted[1:]:
+        inner_part(1, m)
     live = loads[0] >= 1
     refresh = jnp.logical_and(live, flags[0] == 1)
+    first[0].forward()
+    first[1].send(rest)
 
     def squares_of(step, sums):
         rows = pl.ds(pl.multiple_of(step * 16, 16), 16)
@@ -317,21 +362,24 @@
     count = jnp.where(jnp.logical_and(live, me == 0), 1.0, 0.0)
     tile_row = lax.broadcasted_iota(jnp.int32, (8, 128), 0)
     total[0] = jnp.where(tile_row == 0, total_sq, jnp.where(tile_row == 1, count, 0.0))
-    total_copy(0).start()
-
+    total_start(0)
+    first[1].forward()
+    total_next(0)
     first[0].finish()
-    for item in own[:2]:
-        spread_copy(0, *item).start()
-    first[1].forward()
-    for item in own[2:]:
+    for item in own:
         spread_copy(0, *item).start()
     add_power(0, 0)
+    total_next(1)
+    first[1].finish()
+    for item in own[:2]:
+        spread_copy(1, *item).start()
+    total_next(2)
+    add_power(1, 0)
     relay(0)
-    first[1].finish()
-    for item in own:
+    for item in own[2:]:
         spread_copy(1, *item).start()
-    total_next(0)
-    add_power(1, 0)
+    relay(1)
+    total_next(3)
     for m in masks[1:]:
         add_power(0, m)
     gram_a[0] = dot_t(power[0:half, :], power[0:half, :])
@@ -342,30 +390,28 @@
             part2[a, m] = dot(power[a * half : (a + 1) * half, :], g_ref[m])
 
     cross_part(0)
-    total_next(1)
-    relay(1)
-    second[0].send(schedule[0][:2])
+    second[0].send(opening)
+    for m in masks[1:-1]:
+        add_power(1, m)
     for phase in range(bits - 1):
         gram_add(0, phase)
         gram_send(0, phase + 1)
-    second[0].send(schedule[0][2:])
-    total_next(2)
-    for m in masks[1:]:
-        add_power(1, m)
+    add_power(1, masks[-1])
+    total_next(4)
     gram_b[0] = dot_t(power[...], power[half:size, :])
     gram_send(1, 0)
+    second[0].send(rest)
+    cross_part(1)
     gram_add(0, bits - 1)
     panels = half // PANEL
     work[...] = gram_a[bits]
-    panel_steps(work, 0, panels // 2)
-    second[0].forward()
-    cross_part(1)
-    panel_steps(work, panels // 2, panels)
+    panel_steps(work, 0, panels // 4)
     for phase in range(bits - 1):
         gram_add(1, phase)
         gram_send(1, phase + 1)
+    second[0].forward()
     second[1].send(schedule[0])
-    total_next(3)
+    panel_steps(work, panels // 4, panels)
 
     def write_fresh(a, pieces):
         for at in range(0, depth, tile):
@@ -374,15 +420,7 @@
             left = power[0 : (a + 1) * half, rows].T
             value = dot(left, pieces[2]) + dot(left, pieces[1]) + dot(left, pieces[0])
             kept = jnp.where(live, b_ref[rows, columns].astype(F32), 0.0)
-            fresh[a, rows, :] = jnp.where(refresh, value, kept)
-        fresh_out(a).start()
-
-    def fresh_out(a):
-        return pltpu.make_async_copy(fresh.at[a], fresh_hbm.at[:, pl.ds(a * half, half)], out_sem.at[a])
-
-    def rot_out(a):
-        rows = pl.ds(a * half, half)
-        return pltpu.make_async_copy(rot.at[rows], rot_hbm.at[rows], out_sem.at[2 + a])
+            fresh[rows, columns] = jnp.where(refresh, value, kept)
 
     inverse_a = lower_of(work)
     write_fresh(0, pieces_of(inverse_a.T, 3))
@@ -391,26 +429,29 @@
     gram_add(1, bits - 1)
     upper = dot(inverse_a, gram_b[bits, 0:half], HIGHEST)
     work[...] = gram_b[bits, half:size] - dot(upper.T, upper, HIGHEST)
-    panel_steps(work, 0, panels // 2)
+    panel_steps(work, 0, panels * 3 // 8)
     second[1].forward()
-    panel_steps(work, panels // 2, panels)
+    panel_steps(work, panels * 3 // 8, panels)
     inverse_b = lower_of(work)
     mixed = -dot(inverse_b, dot(upper.T, inverse_a, HIGHEST), HIGHEST)
     write_fresh(1, pieces_of(jnp.concatenate([mixed, inverse_b], axis=1).T, 3))
     partly = dot(mixed, part2[0, 0], HIGHEST)
-    for at in range(4, len(peers)):
+    inverse_pair = jnp.concatenate(pieces_of(inverse_b, 2), axis=1)
+    for at in range(5, len(rounds)):
         total_next(at)
-    final = total[len(peers)]
+    final = total[len(rounds)]
     norm = lax.rsqrt(final[0:1, 0:1] / (final[1:2, 0:1] * entries) + 1e-6)
 
     def write_rot(a, turned):
         value = jnp.where(refresh, turned, jnp.where(live, part[a, 0], 0.0)) * norm
         rot[a * half : (a + 1) * half, :] = value
-        rot_out(a).start()
 
     write_rot(0, turned_a)
     second[1].finish()
-    write_rot(1, partly + dot(inverse_b, part2[1, 0], HIGHEST))
+    top, low = pieces_of(part2[1, 0], 2)
+    turned_b = dot(inverse_pair, jnp.concatenate([low, low], axis=0))
+    turned_b = turned_b + dot(inverse_pair, jnp.concatenate([top, top], axis=0))
+    write_rot(1, partly + turned_b)
     for a in range(2):
         first[a].drain()
         second[a].drain()
@@ -419,9 +460,19 @@
         for phase in range(bits):
             for h in range(2):
                 gram_copy(a, phase, h).wait_send()
-        fresh_out(a).wait()
-    for a in range(2):
-        rot_out(a).wait()
+
+
+def write_out(fresh, rot, fresh_hbm, rot_hbm, fresh_sem, rot_sem):
+    depth = fresh.shape[0]
+    extent = depth // PARTS
+    copies = [pltpu.make_async_copy(rot, rot_hbm.at[0], rot_sem.at[0])]
+    for at in range(PARTS):
+        rows = pl.ds(at * extent, extent)
+        copies.append(pltpu.make_async_copy(fresh.at[rows], fresh_hbm.at[0, rows], fresh_sem.at[at]))
+    for item in copies:
+        item.start()
+    for item in copies:
+        item.wait()
 
 
 def on_device(n, experts, grads, basis, loads, flags):
@@ -430,19 +481,17 @@
     half = size // 2
     block = wide // n
     bits = n.bit_length() - 1
-    peers = bits + experts.bit_length() - 1
+    rounds = bits + experts.bit_length() - 1 + (experts == 8)
     moves = 2 * (n - 1)
     anywhere = pl.BlockSpec(memory_space=pl.ANY)
+    vmem = pl.BlockSpec(memory_space=pltpu.VMEM)
     chunk = (half // 2, block)
     dma = pltpu.SemaphoreType.DMA
     new_basis, rotated = pl.pallas_call(
         functools.partial(kernel, n, experts, float(depth * n * wide)),
-        out_shape=(
-            jax.ShapeDtypeStruct((depth, size), F32),
-            jax.ShapeDtypeStruct((size, block), F32),
-        ),
-        in_specs=[anywhere] * 4,
-        out_specs=(anywhere, anywhere),
+        out_shape=(pltpu.VMEM((depth, size), F32), pltpu.VMEM((size, block), F32)),
+        in_specs=[pl.BlockSpec(memory_space=pltpu.HBM)] * 2 + [pl.BlockSpec(memory_space=pltpu.SMEM)] * 2,
+        out_specs=(vmem, vmem),
         scratch_shapes=[
             pltpu.VMEM((n, depth, block), BF16),
             pltpu.VMEM((depth, size), BF16),
@@ -460,21 +509,27 @@
             pltpu.VMEM((bits + 1, size, half), F32),
             pltpu.VMEM((bits, size, half), F32),
             pltpu.VMEM((half, half), F32),
-            pltpu.VMEM((2, depth, half), F32),
-            pltpu.VMEM((size, block), F32),
-            pltpu.VMEM((peers + 1, 8, 128), F32),
-            pltpu.VMEM((peers, 8, 128), F32),
-            pltpu.SMEM((1,), jnp.int32),
-            pltpu.SMEM((1,), jnp.int32),
-            dma((n,)), dma((2,)), dma((2,)), dma((4,)),
+            pltpu.VMEM((rounds + 1, 8, 128), F32),
+            pltpu.VMEM((rounds, 8, 128), F32),
+            dma((n,)), dma((2,)),
             dma((2, moves)), dma((2, moves)), dma((2, moves)), dma((2, moves)), dma((2, moves)), dma((2, moves)),
-            dma((2, bits, 2)), dma((2, bits, 2)), dma((peers,)), dma((peers,)),
+            dma((2, bits, 2)), dma((2, bits, 2)), dma((rounds,)), dma((rounds,)),
         ],
         compiler_params=pltpu.CompilerParams(
-            collective_id=0, has_side_effects=True, vmem_limit_bytes=58 * 1024 * 1024
+            collective_id=0, has_side_effects=True, vmem_limit_bytes=32 * 1024 * 1024
         ),
-    )(grads[0], basis[0], loads, flags)
-    return new_basis[None], rotated[None]
+    )(*[pltpu.with_memory_space_constraint(x, pltpu.HBM) for x in (grads[0], basis[0])], loads, flags)
+    return pl.pallas_call(
+        write_out,
+        out_shape=(
+            jax.ShapeDtypeStruct((1, depth, size), F32),
+            jax.ShapeDtypeStruct((1, size, block), F32),
+        ),
+        in_specs=[vmem] * 2,
+        out_specs=(anywhere, anywhere),
+        scratch_shapes=[dma((PARTS,)), dma((1,))],
+        compiler_params=pltpu.CompilerParams(vmem_limit_bytes=16 * 1024 * 1024),
+    )(new_basis, rotated)
 
 
 def solution(mesh):

time: 72 us -> 66 us (0.917)
  local copies, waits for them, and re-layouts: 3.7 us -> 0 us
  Pallas kernels: 66.2 us -> 63.9 us
    unnamed x4 -> x0, local copies, waits for them, and re-layouts: 3.7 us -> none
    pallas_call x1, Pallas kernels: 66.2 us -> 62.5 us  [on_device(): pl.pallas_call(functools.partial(kernel, n, experts, float(depth * n * wi...]
    pallas_call x0 -> x1, Pallas kernels: none -> 1.44 us  [on_device(): pl.pallas_call(write_out, out_shape=(jax.ShapeDtypeStruct((1, depth, size...]
where the time goes in v3:
time: 66 us; the launch traced here: 65.9 us
  Pallas kernels  63.9 us (97%)
  between operations  1.93 us (3%)
    pallas_call x1, Pallas kernels, on_device(): pl.pallas_call(functools.partial(kernel, n, experts, float(depth * n * wi...  62.5 us
    pallas_call x1, Pallas kernels, on_device(): pl.pallas_call(write_out, out_shape=(jax.ShapeDtypeStruct((1, depth, size...  1.44 us

profile of v3, /device:TPU:0, one launch (start us, length us, event | category | flops | bytes accessed | tf_op | source)
XLA Modules:
  0.0 65.9 jit_solution(13124546261465591771)
XLA Ops:
  1.9 62.5 %shard_map.59 = (f32[1792,256]{1,0:T(8,128)S(1)}, f32[256,512]{1,0:T(8,128)S(1)}) custom-call(bf16[1792,2048]{1,0:T(8,128)(2,1)} %bitcast.2, bf16[1792,256]{1,0:T(8,128)(2,1)} %bitcast.3, s32[1]{0:T(128)S(6)} %copy.6.loads, s32[1]{0:T(128)S(6)} %copy.7.flags), custom_call_target="tpu_custom_call" | custom-call | tf_op jit(solution)/shard_map/pallas_call | solution.py:490
  64.4 1.4 %shard_map.60 = (f32[1,1792,256]{2,1,0:T(8,128)}, f32[1,256,512]{2,1,0:T(8,128)}) custom-call(f32[1792,256]{1,0:T(8,128)S(1)} %get-tuple-element.4.fresh, f32[256,512]{1,0:T(8,128)S(1)} %get-tuple-element.5.rot), custom_call_target="tpu_custom_call" | custom-call | tf_op jit(solution)/shard_map/pallas_call | solution.py:522

commit v4 on v3

--- a/solution.py
+++ b/solution.py
@@ -68,6 +68,25 @@
     work[size - PANEL :, :] = pltpu.roll(full, size - PANEL, 1)
 
 
+def pack(square):
+    size = square.shape[0]
+    q = size // 4
+    lane = lax.broadcasted_iota(jnp.int32, (q, size), 1)
+    second = jnp.where(lane < q, pltpu.roll(square[3 * q :], q, 1), square[q : 2 * q])
+    third = square[2 * q : 3 * q]
+    lane = lane[: q // 2]
+    third = jnp.where(lane < 2 * q, pltpu.roll(third[q // 2 :], 2 * q, 1), third[: q // 2])
+    return jnp.concatenate([square[:q], second, third], axis=0)
+
+
+def unpack(packed):
+    size = packed.shape[1]
+    q = size // 4
+    second, third = packed[q : 2 * q], packed[2 * q :]
+    rows = [packed[:q], second, third, pltpu.roll(third, 2 * q, 1), pltpu.roll(second, size - q, 1)]
+    return jnp.concatenate(rows, axis=0)
+
+
 def panel_steps(work, begin, end):
     def body(step, carry):
         panel_step(work, step)
@@ -87,7 +106,7 @@
     g_ref, b_ref, bt, part, land, full, inner, rough, power, part2, land2,
     gram_a, gram_a_land, gram_b, gram_b_land, work, total, total_land,
     g_sem, b_sem,
-    s_rs, r_rs, s_ag, r_ag, s_rs2, r_rs2, s_gr, r_gr, s_tot, r_tot,
+    s_rs, r_rs, s_ag, r_ag, s_rs2, r_rs2, r_cut, s_gr, r_gr, s_tot, r_tot,
 ):
     _, depth, block = g_ref.shape
     bits = n.bit_length() - 1
@@ -98,6 +117,7 @@
     me = lax.axis_index("row")
     my_expert = lax.axis_index("expert")
     orders = [tuple(range(bits)), tuple(reversed(range(bits)))]
+    cuts = g_sem.shape[1]
 
     def other(index, mask):
         at = index
@@ -134,9 +154,10 @@
         pl.when(inside)(lambda: greet(across))
         greetings = greetings + inside.astype(jnp.int32)
 
-    def load(m):
-        columns = pl.ds(pl.multiple_of(other(me, m) * block, block), block)
-        return pltpu.make_async_copy(g_hbm.at[:, columns], g_ref.at[m], g_sem.at[m])
+    def load(m, cut):
+        width = block // cuts
+        columns = pl.ds(pl.multiple_of(other(me, m) * block + cut * width, width), width)
+        return pltpu.make_async_copy(g_hbm.at[:, columns], g_ref.at[m, :, pl.ds(cut * width, width)], g_sem.at[m, cut])
 
     def load_basis(a):
         columns = pl.ds(a * half, half)
@@ -147,6 +168,9 @@
             src_ref=src, dst_ref=dst, send_sem=send, recv_sem=recv,
             device_id=to, device_id_type=pl.DeviceIdType.MESH,
         )
+
+    def settle(sent, sem):
+        pltpu.make_async_copy(sent, sent, sem).wait()
 
     def strip(h):
         return pl.ds(h * sub, sub)
@@ -166,31 +190,40 @@
             slot[h, phase, there] = len(slot)
 
     class Halving:
-        def __init__(self, a, parts, lands, sends, recvs):
+        def __init__(self, a, parts, lands, sends, recvs, early):
             self.a, self.parts, self.lands, self.sends, self.recvs = a, parts, lands, sends, recvs
+            self.early = early
 
         def make(self, h, phase, m, there):
             at = slot[h, phase, there]
-            return copy(
-                self.parts.at[self.a, m, strip(h)], self.lands.at[self.a, at],
-                self.sends.at[self.a, at], self.recvs.at[self.a, at], partner(orders[h][phase]),
-            )
+            count = cuts if self.early and (h, phase, m, there) in schedule[0][:2] else 1
+            width = block // count
+            return [
+                copy(
+                    self.parts.at[self.a, m, strip(h), pl.ds(cut * width, width)],
+                    self.lands.at[self.a, at, :, pl.ds(cut * width, width)],
+                    self.sends.at[self.a], self.recvs.at[self.a, at] if cut == 0 else r_cut.at[h], partner(orders[h][phase]),
+                )
+                for cut in range(count)
+            ]
 
         def absorb(self, h, phase, m):
-            self.make(h, phase, m | 1 << orders[h][phase], m).wait_recv()
+            for item in self.make(h, phase, m | 1 << orders[h][phase], m):
+                item.wait_recv()
             rows = slice(h * sub, (h + 1) * sub)
             self.parts[self.a, m, rows] = self.parts[self.a, m, rows] + self.lands[self.a, slot[h, phase, m]]
 
         def send(self, moves):
             for move in moves:
-                self.make(*move).start()
+                for item in self.make(*move):
+                    item.start()
 
         def forward(self):
             for phase in range(1, bits):
                 for move in schedule[phase]:
                     for earlier in range(phase):
                         self.absorb(move[0], earlier, move[2])
-                    self.make(*move).start()
+                    self.send([move])
 
         def finish(self):
             for phase in range(bits):
@@ -198,12 +231,10 @@
                     self.absorb(h, phase, 0)
 
         def drain(self):
-            for phase_moves in schedule:
-                for move in phase_moves:
-                    self.make(*move).wait_send()
-
-    first = [Halving(a, part, land, s_rs, r_rs) for a in range(2)]
-    second = [Halving(a, part2, land2, s_rs2, r_rs2) for a in range(2)]
+            settle(self.parts.at[self.a, pl.ds(0, n - 1)], self.sends.at[self.a])
+
+    first = [Halving(a, part, land, s_rs, r_rs, a == 0) for a in range(2)]
+    second = [Halving(a, part2, land2, s_rs2, r_rs2, False) for a in range(2)]
 
     spread = []
     for h in range(2):
@@ -220,7 +251,7 @@
     def spread_copy(a, h, bit, m):
         at = number[h, m | 1 << bit]
         src = part.at[a, 0, strip(h)] if m == 0 else full.at[a, m, strip(h)]
-        return copy(src, full.at[a, m | 1 << bit, strip(h)], s_ag.at[a, at], r_ag.at[a, at], partner(bit))
+        return copy(src, full.at[a, m | 1 << bit, strip(h)], s_ag.at[a], r_ag.at[a, at], partner(bit))
 
     arrived = set()
 
@@ -260,7 +291,7 @@
         rows = pl.ds(h * extent, extent)
         return copy(
             held.at[phase, rows], landed.at[phase, rows],
-            s_gr.at[a, phase, h], r_gr.at[a, phase, h], partner(orders[h][phase]),
+            s_gr.at[a], r_gr.at[a, phase, h], partner(orders[h][phase]),
         )
 
     def gram_send(a, phase):
@@ -276,7 +307,7 @@
             held[phase + 1, rows] = held[phase, rows] + landed[phase, rows]
 
     def total_copy(at):
-        return copy(total.at[at], total_land.at[at], s_tot.at[at], r_tot.at[at], rounds[at][1])
+        return copy(total.at[at], total_land.at[at], s_tot.at[0], r_tot.at[at], rounds[at][1])
 
     def total_start(at):
         if at == len(rounds):
@@ -315,7 +346,8 @@
     wanted = [move[2] for move in schedule[0]] + list(range(n))
     wanted = sorted(range(n), key=wanted.index)
     load_basis(0).start()
-    load(wanted[0]).start()
+    for cut in range(cuts):
+        load(wanted[0], cut).start()
     span = 128 if depth % 128 == 0 else depth
 
     def turn_basis(a):
@@ -325,7 +357,8 @@
     load_basis(0).wait()
     load_basis(1).start()
     for m in wanted[1:]:
-        load(m).start()
+        for cut in range(cuts):
+            load(m, cut).start()
     turn_basis(0)
     pl.semaphore_wait(barrier, greetings)
 
@@ -334,15 +367,22 @@
 
     opening = schedule[0][:2]
     rest = schedule[0][2:]
-    for m in wanted:
-        load(m).wait()
+    for cut in range(cuts):
+        load(wanted[0], cut).wait()
+        columns = slice(cut * (block // cuts), (cut + 1) * (block // cuts))
+        part[0, wanted[0], :, columns] = dot(bt[:half, :], g_ref[wanted[0], :, columns])
+        for move in opening:
+            first[0].make(*move)[cut].start()
+    for m in wanted[1:]:
+        for cut in range(cuts):
+            load(m, cut).wait()
         if m == wanted[-1]:
             load_basis(1).wait()
             turn_basis(1)
             inner_part(1, wanted[0])
             first[1].send(opening)
         inner_part(0, m)
-        first[0].send([move for move in schedule[0] if move[2] == m])
+        first[0].send([move for move in rest if move[2] == m])
     for m in wanted[1:]:
         inner_part(1, m)
     live = loads[0] >= 1
@@ -382,7 +422,7 @@
     total_next(3)
     for m in masks[1:]:
         add_power(0, m)
-    gram_a[0] = dot_t(power[0:half, :], power[0:half, :])
+    gram_a[0] = pack(dot_t(power[0:half, :], power[0:half, :]))
     gram_send(0, 0)
 
     def cross_part(a):
@@ -398,13 +438,14 @@
         gram_send(0, phase + 1)
     add_power(1, masks[-1])
     total_next(4)
-    gram_b[0] = dot_t(power[...], power[half:size, :])
+    both = dot_t(power[...], power[half:size, :])
+    gram_b[0] = jnp.concatenate([both[:half], pack(both[half:])], axis=0)
     gram_send(1, 0)
     second[0].send(rest)
     cross_part(1)
     gram_add(0, bits - 1)
     panels = half // PANEL
-    work[...] = gram_a[bits]
+    work[...] = unpack(gram_a[bits])
     panel_steps(work, 0, panels // 4)
     for phase in range(bits - 1):
         gram_add(1, phase)
@@ -424,14 +465,14 @@
 
     inverse_a = lower_of(work)
     write_fresh(0, pieces_of(inverse_a.T, 3))
+    gram_add(1, bits - 1)
+    upper = dot(inverse_a, gram_b[bits, :half], HIGHEST)
+    work[...] = unpack(gram_b[bits, half:]) - dot(upper.T, upper, HIGHEST)
+    panel_steps(work, 0, panels * 3 // 4)
     second[0].finish()
     turned_a = dot(inverse_a, part2[0, 0], HIGHEST)
-    gram_add(1, bits - 1)
-    upper = dot(inverse_a, gram_b[bits, 0:half], HIGHEST)
-    work[...] = gram_b[bits, half:size] - dot(upper.T, upper, HIGHEST)
-    panel_steps(work, 0, panels * 3 // 8)
     second[1].forward()
-    panel_steps(work, panels * 3 // 8, panels)
+    panel_steps(work, panels * 3 // 4, panels)
     inverse_b = lower_of(work)
     mixed = -dot(inverse_b, dot(upper.T, inverse_a, HIGHEST), HIGHEST)
     write_fresh(1, pieces_of(jnp.concatenate([mixed, inverse_b], axis=1).T, 3))
@@ -455,11 +496,8 @@
     for a in range(2):
         first[a].drain()
         second[a].drain()
-        for item in spread:
-            spread_copy(a, *item).wait_send()
-        for phase in range(bits):
-            for h in range(2):
-                gram_copy(a, phase, h).wait_send()
+        settle(full.at[a, pl.ds(0, n - 1)], s_ag.at[a])
+        settle(grams[a][0].at[pl.ds(0, bits)], s_gr.at[a])
 
 
 def write_out(fresh, rot, fresh_hbm, rot_hbm, fresh_sem, rot_sem):
@@ -483,6 +521,8 @@
     bits = n.bit_length() - 1
     rounds = bits + experts.bit_length() - 1 + (experts == 8)
     moves = 2 * (n - 1)
+    packed = half * 5 // 8
+    cuts = 2 if block % 256 == 0 else 1
     anywhere = pl.BlockSpec(memory_space=pl.ANY)
     vmem = pl.BlockSpec(memory_space=pltpu.VMEM)
     chunk = (half // 2, block)
@@ -504,16 +544,16 @@
             pltpu.VMEM((size, depth), BF16),
             pltpu.VMEM((2, n, half, block), F32),
             pltpu.VMEM((2, moves, *chunk), F32),
-            pltpu.VMEM((bits + 1, half, half), F32),
-            pltpu.VMEM((bits, half, half), F32),
-            pltpu.VMEM((bits + 1, size, half), F32),
-            pltpu.VMEM((bits, size, half), F32),
+            pltpu.VMEM((bits + 1, packed, half), F32),
+            pltpu.VMEM((bits, packed, half), F32),
+            pltpu.VMEM((bits + 1, half + packed, half), F32),
+            pltpu.VMEM((bits, half + packed, half), F32),
             pltpu.VMEM((half, half), F32),
             pltpu.VMEM((rounds + 1, 8, 128), F32),
             pltpu.VMEM((rounds, 8, 128), F32),
-            dma((n,)), dma((2,)),
-            dma((2, moves)), dma((2, moves)), dma((2, moves)), dma((2, moves)), dma((2, moves)), dma((2, moves)),
-            dma((2, bits, 2)), dma((2, bits, 2)), dma((rounds,)), dma((rounds,)),
+            dma((n, cuts)), dma((2,)),
+            dma((2,)), dma((2, moves)), dma((2,)), dma((2, moves)), dma((2,)), dma((2, moves)), dma((2,)),
+            dma((2,)), dma((2, bits, 2)), dma((1,)), dma((rounds,)),
         ],
         compiler_params=pltpu.CompilerParams(
             collective_id=0, has_side_effects=True, vmem_limit_bytes=32 * 1024 * 1024

time: 66 us -> 64.3 us (0.974)
  Pallas kernels: 63.9 us -> 62.2 us
    pallas_call x1, Pallas kernels: 62.5 us -> 60.8 us  [on_device(): pl.pallas_call(functools.partial(kernel, n, experts, float(depth * n * wi...]
where the time goes in v4:
time: 64.3 us; the launch traced here: 64.2 us
  Pallas kernels  62.2 us (97%)
  between operations  1.93 us (3%)
    pallas_call x1, Pallas kernels, on_device(): pl.pallas_call(functools.partial(kernel, n, experts, float(depth * n * wi...  60.8 us
    pallas_call x1, Pallas kernels, on_device(): pl.pallas_call(write_out, out_shape=(jax.ShapeDtypeStruct((1, depth, size...  1.44 us

profile of v4, /device:TPU:0, one launch (start us, length us, event | category | flops | bytes accessed | tf_op | source)
XLA Modules:
  0.0 64.2 jit_solution(11121749928077496015)
XLA Ops:
  1.9 60.8 %shard_map.59 = (f32[1792,256]{1,0:T(8,128)S(1)}, f32[256,512]{1,0:T(8,128)S(1)}) custom-call(bf16[1792,2048]{1,0:T(8,128)(2,1)} %bitcast.2, bf16[1792,256]{1,0:T(8,128)(2,1)} %bitcast.3, s32[1]{0:T(128)S(6)} %copy.6.loads, s32[1]{0:T(128)S(6)} %copy.7.flags), custom_call_target="tpu_custom_call" | custom-call | tf_op jit(solution)/shard_map/pallas_call | solution.py:530
  62.7 1.4 %shard_map.60 = (f32[1,1792,256]{2,1,0:T(8,128)}, f32[1,256,512]{2,1,0:T(8,128)}) custom-call(f32[1792,256]{1,0:T(8,128)S(1)} %get-tuple-element.4.fresh, f32[256,512]{1,0:T(8,128)S(1)} %get-tuple-element.5.rot), custom_call_target="tpu_custom_call" | custom-call | tf_op jit(solution)/shard_map/pallas_call | solution.py:562

commit v5 on v4

--- a/solution.py
+++ b/solution.py
@@ -29,6 +29,11 @@
         pieces.append(x.astype(BF16))
         x = x - pieces[-1].astype(F32)
     return pieces
+
+
+def scale_of(peak):
+    scale = jnp.where(peak > 2.0**10, 2.0**-40, jnp.where(peak < 2.0**-10, 2.0**40, 1.0))
+    return jnp.where(peak > 2.0**35, 2.0**-80, jnp.where(peak < 2.0**-35, 2.0**80, scale))
 
 
 def first_bit(mask, order):
@@ -102,11 +107,11 @@
 
 
 def kernel(
-    n, experts, entries, g_hbm, b_hbm, loads, flags, fresh, rot,
+    n, experts, entries, g_hbm, b_hbm, loads, flags, fresh, rot, pair, cross,
     g_ref, b_ref, bt, part, land, full, inner, rough, power, part2, land2,
     gram_a, gram_a_land, gram_b, gram_b_land, work, total, total_land,
     g_sem, b_sem,
-    s_rs, r_rs, s_ag, r_ag, s_rs2, r_rs2, r_cut, s_gr, r_gr, s_tot, r_tot,
+    s_rs, r_rs, s_ag, r_ag, s_rs2, r_rs2, s_gr, r_gr, s_tot, r_tot,
 ):
     _, depth, block = g_ref.shape
     bits = n.bit_length() - 1
@@ -117,7 +122,7 @@
     me = lax.axis_index("row")
     my_expert = lax.axis_index("expert")
     orders = [tuple(range(bits)), tuple(reversed(range(bits)))]
-    cuts = g_sem.shape[1]
+    cuts = g_sem.shape[0] - n + 1
 
     def other(index, mask):
         at = index
@@ -154,10 +159,12 @@
         pl.when(inside)(lambda: greet(across))
         greetings = greetings + inside.astype(jnp.int32)
 
-    def load(m, cut):
-        width = block // cuts
+    def load(index, cut=0):
+        m = wanted[index]
+        width = block if index else block // cuts
         columns = pl.ds(pl.multiple_of(other(me, m) * block + cut * width, width), width)
-        return pltpu.make_async_copy(g_hbm.at[:, columns], g_ref.at[m, :, pl.ds(cut * width, width)], g_sem.at[m, cut])
+        sem = g_sem.at[cuts - 1 + index if index else cut]
+        return pltpu.make_async_copy(g_hbm.at[:, columns], g_ref.at[m, :, pl.ds(cut * width, width)], sem)
 
     def load_basis(a):
         columns = pl.ds(a * half, half)
@@ -189,10 +196,16 @@
         for h, phase, m, there in phase_moves:
             slot[h, phase, there] = len(slot)
 
+    def stage(h, m):
+        return first_bit(m, orders[h]) % bits
+
+    stages = [stage(h, there) for h, _, there in slot]
+
     class Halving:
         def __init__(self, a, parts, lands, sends, recvs, early):
             self.a, self.parts, self.lands, self.sends, self.recvs = a, parts, lands, sends, recvs
             self.early = early
+            self.landed = set()
 
         def make(self, h, phase, m, there):
             at = slot[h, phase, there]
@@ -202,14 +215,16 @@
                 copy(
                     self.parts.at[self.a, m, strip(h), pl.ds(cut * width, width)],
                     self.lands.at[self.a, at, :, pl.ds(cut * width, width)],
-                    self.sends.at[self.a], self.recvs.at[self.a, at] if cut == 0 else r_cut.at[h], partner(orders[h][phase]),
+                    self.sends.at[self.a], self.recvs.at[self.a, stage(h, there)], partner(orders[h][phase]),
                 )
                 for cut in range(count)
             ]
 
         def absorb(self, h, phase, m):
-            for item in self.make(h, phase, m | 1 << orders[h][phase], m):
-                item.wait_recv()
+            group = stage(h, m)
+            if group not in self.landed:
+                self.landed.add(group)
+                settle(land.at[0, pl.ds(0, stages.count(group))], self.recvs.at[self.a, group])
             rows = slice(h * sub, (h + 1) * sub)
             self.parts[self.a, m, rows] = self.parts[self.a, m, rows] + self.lands[self.a, slot[h, phase, m]]
 
@@ -243,22 +258,28 @@
             for m in list(held):
                 spread.append((h, bit, m))
                 held.append(m | 1 << bit)
-    number = {(h, m | 1 << bit): at for at, (h, bit, m) in enumerate(spread)}
-    source = {(h, m | 1 << bit): (h, bit, m) for h, bit, m in spread}
+    passed = {(h, m) for h, _, m in spread}
+    groups = {}
+    for h, bit, m in spread:
+        there = m | 1 << bit
+        level = bin(there).count("1")
+        groups[h, there] = 2 * level - 2 + ((h, there) not in passed)
+    names = sorted(set(groups.values()))
+    groups = {key: names.index(value) for key, value in groups.items()}
     own = [item for pair in zip(*[[s for s in spread if s[0] == h and s[2] == 0] for h in range(2)]) for item in pair]
     relayed = sorted((s for s in spread if s[2]), key=lambda s: bin(s[2]).count("1"))
 
     def spread_copy(a, h, bit, m):
-        at = number[h, m | 1 << bit]
         src = part.at[a, 0, strip(h)] if m == 0 else full.at[a, m, strip(h)]
-        return copy(src, full.at[a, m | 1 << bit, strip(h)], s_ag.at[a], r_ag.at[a, at], partner(bit))
+        return copy(src, full.at[a, m | 1 << bit, strip(h)], s_ag.at[a], r_ag.at[a, groups[h, m | 1 << bit]], partner(bit))
 
     arrived = set()
 
     def take(a, h, m):
-        if m and (a, h, m) not in arrived:
-            arrived.add((a, h, m))
-            spread_copy(a, *source[h, m]).wait_recv()
+        if m and (a, groups[h, m]) not in arrived:
+            arrived.add((a, groups[h, m]))
+            count = list(groups.values()).count(groups[h, m])
+            settle(land.at[0, pl.ds(0, count)], r_ag.at[a, groups[h, m]])
 
     def relay(a):
         for h, bit, m in relayed:
@@ -267,19 +288,25 @@
 
     tile = 256 if depth % 256 == 0 else 64
     masks = sorted(range(n), key=lambda v: bin(v).count("1"))
+
+    largest = {}
 
     def add_power(a, m):
         for h in range(2):
             take(a, h, m)
         held = part[a, 0] if m == 0 else full[a, m]
         inner[a, m] = held.astype(BF16)
+        peak = jnp.max(jnp.abs(held), axis=0, keepdims=True)
+        largest[a] = peak if m == 0 else jnp.maximum(largest[a], peak)
+        if m == masks[-1]:
+            scale = scale_of(jnp.max(largest[a], axis=1, keepdims=True))
         for at in range(0, depth, tile):
             rows = slice(at, at + tile)
             term = dot_t(inner[a, m], g_ref[m, rows, :])
             if m:
                 term = rough[a, :, rows] + term
             if m == masks[-1]:
-                power[a * half : (a + 1) * half, rows] = term.astype(BF16)
+                power[a * half : (a + 1) * half, rows] = (term * scale).astype(BF16)
             else:
                 rough[a, :, rows] = term
 
@@ -291,7 +318,7 @@
         rows = pl.ds(h * extent, extent)
         return copy(
             held.at[phase, rows], landed.at[phase, rows],
-            s_gr.at[a], r_gr.at[a, phase, h], partner(orders[h][phase]),
+            s_gr.at[a], r_gr.at[a, phase], partner(orders[h][phase]),
         )
 
     def gram_send(a, phase):
@@ -300,11 +327,8 @@
 
     def gram_add(a, phase):
         held, landed = grams[a]
-        extent = held.shape[1] // 2
-        for h in range(2):
-            rows = slice(h * extent, (h + 1) * extent)
-            gram_copy(a, phase, h).wait_recv()
-            held[phase + 1, rows] = held[phase, rows] + landed[phase, rows]
+        settle(landed.at[phase], r_gr.at[a, phase])
+        held[phase + 1] = held[phase] + landed[phase]
 
     def total_copy(at):
         return copy(total.at[at], total_land.at[at], s_tot.at[0], r_tot.at[at], rounds[at][1])
@@ -347,7 +371,7 @@
     wanted = sorted(range(n), key=wanted.index)
     load_basis(0).start()
     for cut in range(cuts):
-        load(wanted[0], cut).start()
+        load(0, cut).start()
     span = 128 if depth % 128 == 0 else depth
 
     def turn_basis(a):
@@ -355,12 +379,10 @@
             bt[a * half : (a + 1) * half, at : at + span] = b_ref[at : at + span, a * half : (a + 1) * half].T
 
     load_basis(0).wait()
+    for index in range(1, n):
+        load(index).start()
     load_basis(1).start()
-    for m in wanted[1:]:
-        for cut in range(cuts):
-            load(m, cut).start()
     turn_basis(0)
-    pl.semaphore_wait(barrier, greetings)
 
     def inner_part(a, m):
         part[a, m] = dot(bt[a * half : (a + 1) * half, :], g_ref[m])
@@ -368,14 +390,16 @@
     opening = schedule[0][:2]
     rest = schedule[0][2:]
     for cut in range(cuts):
-        load(wanted[0], cut).wait()
+        load(0, cut).wait()
         columns = slice(cut * (block // cuts), (cut + 1) * (block // cuts))
         part[0, wanted[0], :, columns] = dot(bt[:half, :], g_ref[wanted[0], :, columns])
+        if cut == 0:
+            pl.semaphore_wait(barrier, greetings)
         for move in opening:
             first[0].make(*move)[cut].start()
-    for m in wanted[1:]:
-        for cut in range(cuts):
-            load(m, cut).wait()
+    for index in range(1, n):
+        load(index).wait()
+        m = wanted[index]
         if m == wanted[-1]:
             load_basis(1).wait()
             turn_basis(1)
@@ -476,23 +500,19 @@
     inverse_b = lower_of(work)
     mixed = -dot(inverse_b, dot(upper.T, inverse_a, HIGHEST), HIGHEST)
     write_fresh(1, pieces_of(jnp.concatenate([mixed, inverse_b], axis=1).T, 3))
-    partly = dot(mixed, part2[0, 0], HIGHEST)
-    inverse_pair = jnp.concatenate(pieces_of(inverse_b, 2), axis=1)
     for at in range(5, len(rounds)):
         total_next(at)
     final = total[len(rounds)]
     norm = lax.rsqrt(final[0:1, 0:1] / (final[1:2, 0:1] * entries) + 1e-6)
 
     def write_rot(a, turned):
-        value = jnp.where(refresh, turned, jnp.where(live, part[a, 0], 0.0)) * norm
-        rot[a * half : (a + 1) * half, :] = value
+        rot[a * half : (a + 1) * half, :] = jnp.where(refresh, turned, jnp.where(live, part[a, 0], 0.0)) * norm
 
     write_rot(0, turned_a)
+    write_rot(1, dot(mixed, part2[0, 0], HIGHEST))
+    pair[...] = jnp.concatenate(pieces_of(jnp.where(refresh, inverse_b * norm, 0.0), 2), axis=1)
     second[1].finish()
-    top, low = pieces_of(part2[1, 0], 2)
-    turned_b = dot(inverse_pair, jnp.concatenate([low, low], axis=0))
-    turned_b = turned_b + dot(inverse_pair, jnp.concatenate([top, top], axis=0))
-    write_rot(1, partly + turned_b)
+    cross[...] = jnp.where(refresh, part2[1, 0], 0.0)
     for a in range(2):
         first[a].drain()
         second[a].drain()
@@ -500,15 +520,20 @@
         settle(grams[a][0].at[pl.ds(0, bits)], s_gr.at[a])
 
 
-def write_out(fresh, rot, fresh_hbm, rot_hbm, fresh_sem, rot_sem):
-    depth = fresh.shape[0]
-    extent = depth // PARTS
-    copies = [pltpu.make_async_copy(rot, rot_hbm.at[0], rot_sem.at[0])]
+def write_out(fresh, rot, pair, cross, fresh_hbm, rot_hbm, last, fresh_sem, rot_sem):
+    extent = fresh.shape[0] // PARTS
+    half = cross.shape[0]
+    copies = [pltpu.make_async_copy(rot.at[pl.ds(0, half)], rot_hbm.at[0, pl.ds(0, half)], rot_sem.at[0])]
     for at in range(PARTS):
         rows = pl.ds(at * extent, extent)
         copies.append(pltpu.make_async_copy(fresh.at[rows], fresh_hbm.at[0, rows], fresh_sem.at[at]))
     for item in copies:
         item.start()
+    top, low = pieces_of(cross[...], 2)
+    turned = dot(pair[...], jnp.concatenate([low, low], axis=0)) + dot(pair[...], jnp.concatenate([top, top], axis=0))
+    last[...] = rot[half:, :] + turned
+    copies.append(pltpu.make_async_copy(last, rot_hbm.at[0, pl.ds(half, half)], rot_sem.at[1]))
+    copies[-1].start()
     for item in copies:
         item.wait()
 
@@ -527,11 +552,14 @@
     vmem = pl.BlockSpec(memory_space=pltpu.VMEM)
     chunk = (half // 2, block)
     dma = pltpu.SemaphoreType.DMA
-    new_basis, rotated = pl.pallas_call(
+    results = pl.pallas_call(
         functools.partial(kernel, n, experts, float(depth * n * wide)),
-        out_shape=(pltpu.VMEM((depth, size), F32), pltpu.VMEM((size, block), F32)),
+        out_shape=(
+            pltpu.VMEM((depth, size), F32), pltpu.VMEM((size, block), F32),
+            pltpu.VMEM((half, size), BF16), pltpu.VMEM((half, block), F32),
+        ),
         in_specs=[pl.BlockSpec(memory_space=pltpu.HBM)] * 2 + [pl.BlockSpec(memory_space=pltpu.SMEM)] * 2,
-        out_specs=(vmem, vmem),
+        out_specs=(vmem, vmem, vmem, vmem),
         scratch_shapes=[
             pltpu.VMEM((n, depth, block), BF16),
             pltpu.VMEM((depth, size), BF16),
@@ -551,9 +579,9 @@
             pltpu.VMEM((half, half), F32),
             pltpu.VMEM((rounds + 1, 8, 128), F32),
             pltpu.VMEM((rounds, 8, 128), F32),
-            dma((n, cuts)), dma((2,)),
-            dma((2,)), dma((2, moves)), dma((2,)), dma((2, moves)), dma((2,)), dma((2, moves)), dma((2,)),
-            dma((2,)), dma((2, bits, 2)), dma((1,)), dma((rounds,)),
+            dma((n - 1 + cuts,)), dma((2,)),
+            dma((2,)), dma((2, bits)), dma((2,)), dma((2, 2 * bits - 1)), dma((2,)), dma((2, bits)),
+            dma((2,)), dma((2, bits)), dma((1,)), dma((rounds,)),
         ],
         compiler_params=pltpu.CompilerParams(
             collective_id=0, has_side_effects=True, vmem_limit_bytes=32 * 1024 * 1024
@@ -565,11 +593,11 @@
             jax.ShapeDtypeStruct((1, depth, size), F32),
             jax.ShapeDtypeStruct((1, size, block), F32),
         ),
-        in_specs=[vmem] * 2,
+        in_specs=[vmem] * 4,
         out_specs=(anywhere, anywhere),
-        scratch_shapes=[dma((PARTS,)), dma((1,))],
+        scratch_shapes=[pltpu.VMEM((half, block), F32), dma((PARTS,)), dma((2,))],
         compiler_params=pltpu.CompilerParams(vmem_limit_bytes=16 * 1024 * 1024),
-    )(new_basis, rotated)
+    )(*results)
 
 
 def solution(mesh):

time: 64.3 us -> 63.6 us (0.989)
  Pallas kernels: 62.2 us -> 61.4 us
    pallas_call x1, Pallas kernels: 60.8 us -> 60 us  [on_device(): pl.pallas_call(functools.partial(kernel, n, experts, float(depth * n * wi...]
where the time goes in v5:
time: 63.6 us; the launch traced here: 63.4 us
  Pallas kernels  61.4 us (97%)
  between operations  1.93 us (3%)
    pallas_call x1, Pallas kernels, on_device(): pl.pallas_call(functools.partial(kernel, n, experts, float(depth * n * wi...  60 us
    pallas_call x1, Pallas kernels, on_device(): pl.pallas_call(write_out, out_shape=(jax.ShapeDtypeStruct((1, depth, size...  1.45 us

profile of v5, /device:TPU:0, one launch (start us, length us, event | category | flops | bytes accessed | tf_op | source)
XLA Modules:
  0.0 63.4 jit_solution(14412989349198869855)
XLA Ops:
  1.9 60.0 %shard_map.59 = (f32[1792,256]{1,0:T(8,128)S(1)}, f32[256,512]{1,0:T(8,128)S(1)}, bf16[128,256]{1,0:T(8,128)(2,1)S(1)}, f32[128,512]{1,0:T(8,128)S(1)}) custom-call(bf16[1792,2048]{1,0:T(8,128)(2,1)} %bitcast.2, bf16[1792,256]{1,0:T(8,128)(2,1)} %bitcast.3, s32[1]{0:T(128)S(6)} %copy.6.loads, s32[1]{0:T(128)S(6)} %copy.7.flags), custom_call_target="tpu_custom_call" | custom-call | tf_op jit(solution)/shard_map/pallas_call | solution.py:555
  61.9 1.4 %shard_map.60 = (f32[1,1792,256]{2,1,0:T(8,128)}, f32[1,256,512]{2,1,0:T(8,128)}) custom-call(f32[1792,256]{1,0:T(8,128)S(1)} %get-tuple-element.6.fresh, f32[256,512]{1,0:T(8,128)S(1)} %get-tuple-element.7.rot, bf16[128,256]{1,0:T(8,128)(2,1)S(1)} %get-tuple-element.8.pair, f32[128,512]{1,0:T(8,128)S(1)} %get-tuple-element.9.cross), custom_call_target="tpu_custom_call" | custom-call | tf_op jit(solution)/shard_map/pallas_call | solution.py:590

commit v6 on v5

--- a/solution.py
+++ b/solution.py
@@ -424,8 +424,8 @@
     sums = lax.fori_loop(0, depth // 16, squares_of, jnp.zeros((16, block), F32))
     total_sq = jnp.where(live, jnp.sum(sums), 0.0)
     count = jnp.where(jnp.logical_and(live, me == 0), 1.0, 0.0)
-    tile_row = lax.broadcasted_iota(jnp.int32, (8, 128), 0)
-    total[0] = jnp.where(tile_row == 0, total_sq, jnp.where(tile_row == 1, count, 0.0))
+    lane = lax.broadcasted_iota(jnp.int32, (1, 128), 1)
+    total[0] = jnp.where(lane == 0, total_sq, jnp.where(lane == 1, count, 0.0))
     total_start(0)
     first[1].forward()
     total_next(0)
@@ -474,8 +474,9 @@
     for phase in range(bits - 1):
         gram_add(1, phase)
         gram_send(1, phase + 1)
+    second[1].send(opening)
     second[0].forward()
-    second[1].send(schedule[0])
+    second[1].send(rest)
     panel_steps(work, panels // 4, panels)
 
     def write_fresh(a, pieces):
@@ -492,18 +493,18 @@
     gram_add(1, bits - 1)
     upper = dot(inverse_a, gram_b[bits, :half], HIGHEST)
     work[...] = unpack(gram_b[bits, half:]) - dot(upper.T, upper, HIGHEST)
-    panel_steps(work, 0, panels * 3 // 4)
+    panel_steps(work, 0, panels * 5 // 8)
+    second[1].forward()
+    panel_steps(work, panels * 5 // 8, panels)
     second[0].finish()
     turned_a = dot(inverse_a, part2[0, 0], HIGHEST)
-    second[1].forward()
-    panel_steps(work, panels * 3 // 4, panels)
     inverse_b = lower_of(work)
     mixed = -dot(inverse_b, dot(upper.T, inverse_a, HIGHEST), HIGHEST)
     write_fresh(1, pieces_of(jnp.concatenate([mixed, inverse_b], axis=1).T, 3))
     for at in range(5, len(rounds)):
         total_next(at)
     final = total[len(rounds)]
-    norm = lax.rsqrt(final[0:1, 0:1] / (final[1:2, 0:1] * entries) + 1e-6)
+    norm = lax.rsqrt(final[0:1, 0:1] / (final[0:1, 1:2] * entries) + 1e-6)
 
     def write_rot(a, turned):
         rot[a * half : (a + 1) * half, :] = jnp.where(refresh, turned, jnp.where(live, part[a, 0], 0.0)) * norm
@@ -577,8 +578,8 @@
             pltpu.VMEM((bits + 1, half + packed, half), F32),
             pltpu.VMEM((bits, half + packed, half), F32),
             pltpu.VMEM((half, half), F32),
-            pltpu.VMEM((rounds + 1, 8, 128), F32),
-            pltpu.VMEM((rounds, 8, 128), F32),
+            pltpu.VMEM((rounds + 1, 1, 128), F32),
+            pltpu.VMEM((rounds, 1, 128), F32),
             dma((n - 1 + cuts,)), dma((2,)),
             dma((2,)), dma((2, bits)), dma((2,)), dma((2, 2 * bits - 1)), dma((2,)), dma((2, bits)),
             dma((2,)), dma((2, bits)), dma((1,)), dma((rounds,)),

time: 63.6 us -> 63.6 us (level)
  no operation moved by 1% of the time
where the time goes in v6:
time: 63.6 us; the launch traced here: 63.4 us
  Pallas kernels  61.4 us (97%)
  between operations  1.93 us (3%)
    pallas_call x1, Pallas kernels, on_device(): pl.pallas_call(functools.partial(kernel, n, experts, float(depth * n * wi...  60 us
    pallas_call x1, Pallas kernels, on_device(): pl.pallas_call(write_out, out_shape=(jax.ShapeDtypeStruct((1, depth, size...  1.45 us

profile of v6, /device:TPU:0, one launch (start us, length us, event | category | flops | bytes accessed | tf_op | source)
XLA Modules:
  0.0 63.4 jit_solution(1087442960972450359)
XLA Ops:
  1.9 60.0 %shard_map.59 = (f32[1792,256]{1,0:T(8,128)S(1)}, f32[256,512]{1,0:T(8,128)S(1)}, bf16[128,256]{1,0:T(8,128)(2,1)S(1)}, f32[128,512]{1,0:T(8,128)S(1)}) custom-call(bf16[1792,2048]{1,0:T(8,128)(2,1)} %bitcast.2, bf16[1792,256]{1,0:T(8,128)(2,1)} %bitcast.3, s32[1]{0:T(128)S(6)} %copy.6.loads, s32[1]{0:T(128)S(6)} %copy.7.flags), custom_call_target="tpu_custom_call" | custom-call | tf_op jit(solution)/shard_map/pallas_call | solution.py:556
  61.9 1.4 %shard_map.60 = (f32[1,1792,256]{2,1,0:T(8,128)}, f32[1,256,512]{2,1,0:T(8,128)}) custom-call(f32[1792,256]{1,0:T(8,128)S(1)} %get-tuple-element.6.fresh, f32[256,512]{1,0:T(8,128)S(1)} %get-tuple-element.7.rot, bf16[128,256]{1,0:T(8,128)(2,1)S(1)} %get-tuple-element.8.pair, f32[128,512]{1,0:T(8,128)S(1)} %get-tuple-element.9.cross), custom_call_target="tpu_custom_call" | custom-call | tf_op jit(solution)/shard_map/pallas_call | solution.py:591

commit v7 on v6

--- a/solution.py
+++ b/solution.py
@@ -512,8 +512,13 @@
     write_rot(0, turned_a)
     write_rot(1, dot(mixed, part2[0, 0], HIGHEST))
     pair[...] = jnp.concatenate(pieces_of(jnp.where(refresh, inverse_b * norm, 0.0), 2), axis=1)
-    second[1].finish()
-    cross[...] = jnp.where(refresh, part2[1, 0], 0.0)
+    settle(land.at[0, pl.ds(0, stages.count(0))], r_rs2.at[1, 0])
+    for h in range(2):
+        rows = slice(h * sub, (h + 1) * sub)
+        value = part2[1, 0, rows]
+        for phase in range(bits):
+            value = value + land2[1, slot[h, phase, 0]]
+        cross[rows, :] = jnp.where(refresh, value, 0.0)
     for a in range(2):
         first[a].drain()
         second[a].drain()

time: 63.6 us -> 63.5 us (level)
  no operation moved by 1% of the time
where the time goes in v7:
time: 63.5 us; the launch traced here: 63.4 us
  Pallas kernels  61.4 us (97%)
  between operations  1.93 us (3%)
    pallas_call x1, Pallas kernels, on_device(): pl.pallas_call(functools.partial(kernel, n, experts, float(depth * n * wi...  60 us
    pallas_call x1, Pallas kernels, on_device(): pl.pallas_call(write_out, out_shape=(jax.ShapeDtypeStruct((1, depth, size...  1.45 us

profile of v7, /device:TPU:0, one launch (start us, length us, event | category | flops | bytes accessed | tf_op | source)
XLA Modules:
  0.0 63.4 jit_solution(1063132462929352728)
XLA Ops:
  1.9 60.0 %shard_map.59 = (f32[1792,256]{1,0:T(8,128)S(1)}, f32[256,512]{1,0:T(8,128)S(1)}, bf16[128,256]{1,0:T(8,128)(2,1)S(1)}, f32[128,512]{1,0:T(8,128)S(1)}) custom-call(bf16[1792,2048]{1,0:T(8,128)(2,1)} %bitcast.2, bf16[1792,256]{1,0:T(8,128)(2,1)} %bitcast.3, s32[1]{0:T(128)S(6)} %copy.6.loads, s32[1]{0:T(128)S(6)} %copy.7.flags), custom_call_target="tpu_custom_call" | custom-call | tf_op jit(solution)/shard_map/pallas_call | solution.py:561
  61.9 1.4 %shard_map.60 = (f32[1,1792,256]{2,1,0:T(8,128)}, f32[1,256,512]{2,1,0:T(8,128)}) custom-call(f32[1792,256]{1,0:T(8,128)S(1)} %get-tuple-element.6.fresh, f32[256,512]{1,0:T(8,128)S(1)} %get-tuple-element.7.rot, bf16[128,256]{1,0:T(8,128)(2,1)S(1)} %get-tuple-element.8.pair, f32[128,512]{1,0:T(8,128)S(1)} %get-tuple-element.9.cross), custom_call_target="tpu_custom_call" | custom-call | tf_op jit(solution)/shard_map/pallas_call | solution.py:596

commit v8 on v6

--- a/solution.py
+++ b/solution.py
@@ -462,8 +462,9 @@
         gram_send(0, phase + 1)
     add_power(1, masks[-1])
     total_next(4)
-    both = dot_t(power[...], power[half:size, :])
-    gram_b[0] = jnp.concatenate([both[:half], pack(both[half:])], axis=0)
+    gram_b[0, :half] = dot_t(power[:half, :], power[half:size, :])
+    gram_b_square = dot_t(power[half:size, :], power[half:size, :])
+    gram_b[0, half:] = pack(gram_b_square)
     gram_send(1, 0)
     second[0].send(rest)
     cross_part(1)

time: 63.6 us -> 63.6 us (level)
  no operation moved by 1% of the time
where the time goes in v8:
time: 63.6 us; the launch traced here: 63.4 us
  Pallas kernels  61.5 us (97%)
  between operations  1.93 us (3%)
    pallas_call x1, Pallas kernels, on_device(): pl.pallas_call(functools.partial(kernel, n, experts, float(depth * n * wi...  60 us
    pallas_call x1, Pallas kernels, on_device(): pl.pallas_call(write_out, out_shape=(jax.ShapeDtypeStruct((1, depth, size...  1.45 us

profile of v8, /device:TPU:0, one launch (start us, length us, event | category | flops | bytes accessed | tf_op | source)
XLA Modules:
  0.0 63.4 jit_solution(3963572763397549182)
XLA Ops:
  1.9 60.0 %shard_map.59 = (f32[1792,256]{1,0:T(8,128)S(1)}, f32[256,512]{1,0:T(8,128)S(1)}, bf16[128,256]{1,0:T(8,128)(2,1)S(1)}, f32[128,512]{1,0:T(8,128)S(1)}) custom-call(bf16[1792,2048]{1,0:T(8,128)(2,1)} %bitcast.2, bf16[1792,256]{1,0:T(8,128)(2,1)} %bitcast.3, s32[1]{0:T(128)S(6)} %copy.6.loads, s32[1]{0:T(128)S(6)} %copy.7.flags), custom_call_target="tpu_custom_call" | custom-call | tf_op jit(solution)/shard_map/pallas_call | solution.py:557
  61.9 1.4 %shard_map.60 = (f32[1,1792,256]{2,1,0:T(8,128)}, f32[1,256,512]{2,1,0:T(8,128)}) custom-call(f32[1792,256]{1,0:T(8,128)S(1)} %get-tuple-element.6.fresh, f32[256,512]{1,0:T(8,128)S(1)} %get-tuple-element.7.rot, bf16[128,256]{1,0:T(8,128)(2,1)S(1)} %get-tuple-element.8.pair, f32[128,512]{1,0:T(8,128)S(1)} %get-tuple-element.9.cross), custom_call_target="tpu_custom_call" | custom-call | tf_op jit(solution)/shard_map/pallas_call | solution.py:592
